TPU v7x, 128 devices: a whole 4x4x4 slice. The times are simulated.
128 devices in a mesh: data: 1, inner: 16 (over z, y), stage: 8 (over x, core).
Axes of the slice: x: 4, y: 4, z: 4, core: 2. Of those that a mesh axis runs over, the one named last changes fastest.
Arguments:
- x_tokens: bfloat16 [128, 32, 1024], P(('data', 'stage', 'inner'))
- g_cotan: bfloat16 [128, 32, 1024], P(('data', 'stage', 'inner'))
- w_up: bfloat16 [2, 8, 1024, 4096], P(None, ('data', 'stage'), None, 'inner')
- w_down: bfloat16 [2, 8, 4096, 1024], P(None, ('data', 'stage'), 'inner')
Outputs:
- output 1: bfloat16 [128, 32, 1024], P(('data', 'stage', 'inner'))
- output 2: bfloat16 [128, 32, 1024], P(('data', 'stage', 'inner'))
- output 3: float32 [2, 8, 1024, 4096], P(None, ('data', 'stage'), None, 'inner')
- output 4: float32 [2, 8, 4096, 1024], P(None, ('data', 'stage'), 'inner')
All inputs are finite; a program needn't handle non-finite values.
Results may differ from a plain program's by a relative error of at most 0.02.
Values are sent between devices in bfloat16 or wider.
A program may use at most 1 GiB of HBM per device.

v0:
```python
import jax
import jax.numpy as jnp
from jax import lax
from jax.sharding import PartitionSpec as P


def gelu_pair(pre_act):
    normal_cdf = 0.5 * (1.0 + lax.erf(pre_act * 0.7071067811865476))
    normal_pdf = jnp.exp(-0.5 * pre_act * pre_act) * 0.3989422804014327
    return pre_act * normal_cdf, normal_cdf + pre_act * normal_pdf


def layer_fwd(h_in, w_one, w_two):
    pre_act = jnp.dot(h_in, w_one, preferred_element_type=jnp.float32)
    act_val = gelu_pair(pre_act)[0].astype(jnp.bfloat16)
    branch = jnp.dot(act_val, w_two, preferred_element_type=jnp.float32)
    return (h_in.astype(jnp.float32) + branch).astype(jnp.bfloat16)


def layer_bwd(h_in, w_one, w_two, g_out):
    pre_act = jnp.dot(h_in, w_one, preferred_element_type=jnp.float32)
    gelu_val, gelu_grad = gelu_pair(pre_act)
    act_val = gelu_val.astype(jnp.bfloat16)
    d_act = lax.dot_general(g_out, w_two, (((1,), (1,)), ((), ())), preferred_element_type=jnp.float32)
    d_pre = (d_act * gelu_grad).astype(jnp.bfloat16)
    grad_one = lax.dot_general(h_in, d_pre, (((0,), (0,)), ((), ())), preferred_element_type=jnp.float32)
    grad_two = lax.dot_general(act_val, g_out, (((0,), (0,)), ((), ())), preferred_element_type=jnp.float32)
    back_term = lax.dot_general(d_pre, w_one, (((1,), (1,)), ((), ())), preferred_element_type=jnp.float32)
    g_in = (g_out.astype(jnp.float32) + back_term).astype(jnp.bfloat16)
    return g_in, grad_one, grad_two


def solution(mesh):
    n_stage = mesh.shape['stage']
    tok_spec = P(('data', 'stage', 'inner'))
    up_spec = P(None, ('data', 'stage'), None, 'inner')
    down_spec = P(None, ('data', 'stage'), 'inner', None)
    fwd_perm = [(src_idx, (src_idx + 1) % n_stage) for src_idx in range(n_stage)]
    bwd_perm = [(src_idx, (src_idx - 1) % n_stage) for src_idx in range(n_stage)]

    def device_step(x_loc, g_loc, w_up, w_down):
        n_virt = w_up.shape[0]
        group_layers = w_up.shape[1]
        d_model = x_loc.shape[2]
        stage_idx = lax.axis_index('stage')
        is_first = stage_idx == 0
        is_last = stage_idx == n_stage - 1
        x_col = lax.all_gather(x_loc, 'stage', axis=0, tiled=True)
        g_col = lax.all_gather(g_loc, 'stage', axis=0, tiled=True)
        n_micro = x_col.shape[0]
        tick_ids = jnp.arange(n_micro + n_stage - 1)
        act_zero = jnp.zeros(x_loc.shape[1:], x_loc.dtype)
        stash_list = []
        act_buf = x_col
        for virt_idx in range(n_virt):
            up_full = lax.all_gather(w_up[virt_idx], 'inner', axis=2, tiled=True)
            down_full = lax.all_gather(w_down[virt_idx], 'inner', axis=1, tiled=True)

            def fwd_tick(loop_state, tick_idx):
                buf_in, recv_act, saved_ins = loop_state
                micro_idx = tick_idx - stage_idx
                is_valid = (micro_idx >= 0) & (micro_idx < n_micro)
                buf_slot = jnp.clip(micro_idx, 0, n_micro - 1)
                from_buf = lax.dynamic_index_in_dim(buf_in, buf_slot, 0, keepdims=False)
                h_act = jnp.where(is_first, from_buf, recv_act)
                layer_ins = []
                for layer_idx in range(group_layers):
                    layer_ins.append(h_act)
                    h_act = layer_fwd(h_act, up_full[layer_idx], down_full[layer_idx])
                old_ins = lax.dynamic_index_in_dim(saved_ins, buf_slot, 0, keepdims=False)
                new_ins = jnp.where(is_valid, jnp.stack(layer_ins), old_ins)
                saved_ins = lax.dynamic_update_index_in_dim(saved_ins, new_ins, buf_slot, 0)
                sent_act = lax.ppermute(h_act, 'stage', fwd_perm)
                done_idx = tick_idx - (n_stage - 1)
                done_slot = jnp.clip(done_idx, 0, n_micro - 1)
                prev_val = lax.dynamic_index_in_dim(buf_in, done_slot, 0, keepdims=False)
                keep_new = is_first & (done_idx >= 0)
                buf_in = lax.dynamic_update_index_in_dim(buf_in, jnp.where(keep_new, sent_act, prev_val), done_slot, 0)
                return (buf_in, sent_act, saved_ins), None

            saved_init = jnp.zeros((n_micro, group_layers) + x_loc.shape[1:], x_loc.dtype)
            end_state = lax.scan(fwd_tick, (act_buf, act_zero, saved_init), tick_ids)[0]
            act_buf = end_state[0]
            stash_list.append(end_state[2])
        y_src = jnp.where(is_first, act_buf, jnp.zeros_like(act_buf))
        y_loc = lax.psum_scatter(y_src, 'stage', scatter_dimension=0, tiled=True)

        grad_buf = g_col
        up_out = [None] * n_virt
        down_out = [None] * n_virt
        for virt_idx in reversed(range(n_virt)):
            up_full = lax.all_gather(w_up[virt_idx], 'inner', axis=2, tiled=True)
            down_full = lax.all_gather(w_down[virt_idx], 'inner', axis=1, tiled=True)
            d_ff = up_full.shape[2]
            saved_ins = stash_list[virt_idx]

            def bwd_tick(loop_state, tick_idx):
                buf_in, recv_grad, acc_one, acc_two = loop_state
                micro_idx = tick_idx - (n_stage - 1 - stage_idx)
                is_valid = (micro_idx >= 0) & (micro_idx < n_micro)
                buf_slot = jnp.clip(micro_idx, 0, n_micro - 1)
                from_buf = lax.dynamic_index_in_dim(buf_in, buf_slot, 0, keepdims=False)
                g_act = jnp.where(is_last, from_buf, recv_grad)
                g_act = jnp.where(is_valid, g_act, jnp.zeros_like(g_act))
                layer_ins = lax.dynamic_index_in_dim(saved_ins, buf_slot, 0, keepdims=False)
                acc_one = list(acc_one)
                acc_two = list(acc_two)
                for layer_idx in reversed(range(group_layers)):
                    g_act, grad_one, grad_two = layer_bwd(layer_ins[layer_idx], up_full[layer_idx], down_full[layer_idx], g_act)
                    acc_one[layer_idx] = acc_one[layer_idx] + grad_one
                    acc_two[layer_idx] = acc_two[layer_idx] + grad_two
                sent_grad = lax.ppermute(g_act, 'stage', bwd_perm)
                done_idx = tick_idx - (n_stage - 1)
                done_slot = jnp.clip(done_idx, 0, n_micro - 1)
                prev_val = lax.dynamic_index_in_dim(buf_in, done_slot, 0, keepdims=False)
                keep_new = is_last & (done_idx >= 0)
                buf_in = lax.dynamic_update_index_in_dim(buf_in, jnp.where(keep_new, sent_grad, prev_val), done_slot, 0)
                return (buf_in, sent_grad, acc_one, acc_two), None

            acc_init_one = [jnp.zeros((d_model, d_ff), jnp.float32) for layer_idx in range(group_layers)]
            acc_init_two = [jnp.zeros((d_ff, d_model), jnp.float32) for layer_idx in range(group_layers)]
            end_state = lax.scan(bwd_tick, (grad_buf, act_zero, acc_init_one, acc_init_two), tick_ids)[0]
            grad_buf = end_state[0]
            up_out[virt_idx] = lax.psum_scatter(jnp.stack(end_state[2]), 'inner', scatter_dimension=2, tiled=True)
            down_out[virt_idx] = lax.psum_scatter(jnp.stack(end_state[3]), 'inner', scatter_dimension=1, tiled=True)
        dx_src = jnp.where(is_last, grad_buf, jnp.zeros_like(grad_buf))
        dx_loc = lax.psum_scatter(dx_src, 'stage', scatter_dimension=0, tiled=True)
        return y_loc, dx_loc, jnp.stack(up_out), jnp.stack(down_out)

    return jax.shard_map(device_step, mesh=mesh, in_specs=(tok_spec, tok_spec, up_spec, down_spec), out_specs=(tok_spec, tok_spec, up_spec, down_spec), check_vma=False)
```

profile of v0, /device:TPU:8, one launch (start us, length us, event | category | flops | bytes accessed | tf_op | source)
XLA Modules:
  0.0 2242.2 jit_solution(14879059542616040947)
XLA Ops:
  39.8 49.4 %all-gather.9.cloned.1.call-done = bf16[1,1,1024,4096]{3,2,1,0:T(8,128)(2,1)} async-done(((bf16[1,1,1024,256]{3,2,1,0:T(8,128)(2,1)}), bf16[1,1,1024,4096]{3,2,1,0:T(8,128)(2,1)}) %all-gather.9.cloned.1.call-update) | async-done | bytes 8388624 | tf_op jit(solution)/shard_map/all_gather | solution.py:56
  89.2 72.4 %all-gather.11.cloned.1.call-done = bf16[1,1,4096,1024]{3,2,1,0:T(8,128)(2,1)} async-done(((bf16[1,1,256,1024]{3,2,1,0:T(8,128)(2,1)}), bf16[1,1,4096,1024]{3,2,1,0:T(8,128)(2,1)}) %all-gather.11.cloned.1.call-update) | async-done | bytes 8388624 | tf_op jit(solution)/shard_map/all_gather | solution.py:57
  161.7 224.5 %while.70 = (s32[]{:T(128)}, bf16[8,32,1024]{2,1,0:T(8,128)(2,1)S(1)}, bf16[32,1024]{1,0:T(8,128)(2,1)S(1)}, bf16[8,1,32,1024]{3,2,1,0:T(8,128)(2,1)S(1)}, s32[1...) while((s32[]{:T(128)}, ...), condition=%wide.region_1.2_spmd, body=%wide.region_0.1_spmd.sunk | while | flops 537788416 | bytes 18221364 | solution.py:82
  387.0 224.5 %while.71 = (s32[]{:T(128)}, bf16[8,32,1024]{2,1,0:T(8,128)(2,1)S(1)}, bf16[32,1024]{1,0:T(8,128)(2,1)S(1)}, bf16[8,1,32,1024]{3,2,1,0:T(8,128)(2,1)S(1)}, s32[1...) while((s32[]{:T(128)}, ...), condition=%wide.region_3.4_spmd, body=%wide.region_2.3_spmd.sunk | while | flops 537788416 | bytes 18221364 | solution.py:82
  612.3 605.7 %while.72 = (s32[]{:T(128)}, bf16[8,32,1024]{2,1,0:T(8,128)(2,1)S(1)}, bf16[32,1024]{1,0:T(8,128)(2,1)S(1)}, f32[1024,4096]{1,0:T(8,128)}, f32[4096,1024]{1,0:T(...) while((s32[]{:T(128)}, ...), condition=%wide.region_6.7_spmd.clone, body=%wide.region_5.6_spmd.clone.sunk | while | flops 1361117184 | bytes 154534304 | solution.py:122
  654.5 13.9 select_add_fusion.8
  668.3 13.9 select_add_fusion.9
  695.2 13.9 select_add_fusion.8
  736.0 13.9 select_add_fusion.8
  749.8 13.9 select_add_fusion.9
  776.7 13.9 select_add_fusion.8
  817.5 13.9 select_add_fusion.8
  859.2 13.9 select_add_fusion.8
  873.0 13.9 select_add_fusion.9
  904.0 13.9 select_add_fusion.8
  917.9 13.9 select_add_fusion.9
  944.8 13.9 select_add_fusion.8
  958.7 13.9 select_add_fusion.9
  985.5 13.9 select_add_fusion.8
  999.4 13.9 select_add_fusion.9
  1026.3 13.9 select_add_fusion.8
  1040.2 13.9 select_add_fusion.9
  1067.0 13.9 select_add_fusion.8
  1080.9 13.9 select_add_fusion.9
  1107.8 13.9 select_add_fusion.8
  1121.7 13.9 select_add_fusion.9
  1148.5 13.9 select_add_fusion.8
  1162.4 13.9 select_add_fusion.9
  1190.2 13.9 select_add_fusion.8
  1204.1 13.9 select_add_fusion.9
  1218.1 611.1 %while.73 = (s32[]{:T(128)}, bf16[8,32,1024]{2,1,0:T(8,128)(2,1)S(1)}, bf16[32,1024]{1,0:T(8,128)(2,1)S(1)}, f32[1024,4096]{1,0:T(8,128)}, f32[4096,1024]{1,0:T(...) while((s32[]{:T(128)}, ...), condition=%wide.region_8.9_spmd.clone, body=%wide.region_7.8_spmd.clone.sunk | while | flops 1361117184 | bytes 154534304 | solution.py:122
  1265.6 13.9 select_add_fusion.10
  1279.5 13.9 select_add_fusion.11
  1306.4 13.9 select_add_fusion.10
  1320.3 13.9 select_add_fusion.11
  1347.2 13.9 select_add_fusion.10
  1361.2 13.9 select_add_fusion.11
  1388.1 13.9 select_add_fusion.10
  1402.0 13.9 select_add_fusion.11
  1428.9 13.9 select_add_fusion.10
  1442.8 13.9 select_add_fusion.11
  1469.7 13.9 select_add_fusion.10
  1483.6 13.9 select_add_fusion.11
  1511.5 13.9 select_add_fusion.10
  1525.4 13.9 select_add_fusion.11
  1556.4 13.9 select_add_fusion.10
  1570.3 13.9 select_add_fusion.11
  1597.3 13.9 select_add_fusion.10
  1611.2 13.9 select_add_fusion.11
  1638.1 13.9 select_add_fusion.10
  1652.0 13.9 select_add_fusion.11
  1678.9 13.9 select_add_fusion.10
  1692.9 13.9 select_add_fusion.11
  1719.8 13.9 select_add_fusion.10
  1733.7 13.9 select_add_fusion.11
  1760.6 13.9 select_add_fusion.10
  1774.5 13.9 select_add_fusion.11
  1801.4 13.9 select_add_fusion.10
  1815.3 13.9 select_add_fusion.11
  1832.9 108.6 %reduce-scatter.11.cloned.1.call-done = f32[1,1024,256]{2,1,0:T(8,128)} async-done(((f32[1,1024,4096]{2,1,0:T(8,128)}), f32[1,1024,256]{2,1,0:T(8,128)}) %reduce-scatter.11.cloned.1.call-update) | async-done | bytes 1048592 | tf_op jit(solution)/shard_map/reduce_scatter | solution.py:124
  1944.5 110.6 %reduce-scatter.17.cloned.1.call-done = f32[1,256,1024]{2,1,0:T(8,128)} async-done(((f32[1,4096,1024]{2,1,0:T(8,128)}), f32[1,256,1024]{2,1,0:T(8,128)}) %reduce-scatter.17.cloned.1.call-update) | async-done | bytes 1048592 | tf_op jit(solution)/shard_map/reduce_scatter | solution.py:125
  2055.1 113.6 %reduce-scatter.15.cloned.1.call-done = f32[1,256,1024]{2,1,0:T(8,128)} async-done(((f32[1,4096,1024]{2,1,0:T(8,128)}), f32[1,256,1024]{2,1,0:T(8,128)}) %reduce-scatter.15.cloned.1.call-update) | async-done | bytes 1048592 | tf_op jit(solution)/shard_map/reduce_scatter | solution.py:125
  2171.7 30.7 %reduce-scatter.7.cloned.1.call-done = bf16[1,32,1024]{2,1,0:T(8,128)(2,1)} async-done(((bf16[8,32,1024]{2,1,0:T(8,128)(2,1)}), bf16[1,32,1024]{2,1,0:T(8,128)(2,1)}) %reduce-scatter.7.cloned.1.call-update) | async-done | bytes 65552 | tf_op jit(solution)/shard_map/reduce_scatter | solution.py:86
  2202.4 32.9 %reduce-scatter.9.cloned.1.call-done = bf16[1,32,1024]{2,1,0:T(8,128)(2,1)} async-done(((bf16[8,32,1024]{2,1,0:T(8,128)(2,1)}), bf16[1,32,1024]{2,1,0:T(8,128)(2,1)}) %reduce-scatter.9.cloned.1.call-update) | async-done | bytes 65552 | tf_op jit(solution)/shard_map/reduce_scatter | solution.py:127
  (808 shorter events, 888.8 us)
Async XLA Ops:
  7.2 82.0 %all-gather.9.cloned.1.call-start = ((), (), s32[]{:S(2)}) async-start(), calls=%async_computation.12 | async-start | bytes 8912896 | tf_op jit(solution)/shard_map/all_gather | solution.py:56
  9.5 152.2 %all-gather.11.cloned.1.call-start = ((), (), s32[]{:S(2)}) async-start(), calls=%async_computation.13 | async-start | bytes 8912896 | tf_op jit(solution)/shard_map/all_gather | solution.py:57
  11.8 374.5 %all-gather.13.cloned.1.call-start = ((), (), s32[]{:S(2)}) async-start(), calls=%async_computation.14 | async-start | bytes 8912896 | tf_op jit(solution)/shard_map/all_gather | solution.py:56
  12.5 373.8 %all-gather.15.cloned.1.call-start = ((), (), s32[]{:S(2)}) async-start(), calls=%async_computation.15 | async-start | bytes 8912896 | tf_op jit(solution)/shard_map/all_gather | solution.py:57
  13.1 1819.8 %reduce-scatter.13.cloned.1.call-start = ((), (), s32[]{:S(2)}) async-start(), calls=%async_computation.9 | async-start | bytes 17825792 | tf_op jit(solution)/shard_map/reduce_scatter | solution.py:124
  171.7 4.9 collective-permute-start
  186.7 4.9 collective-permute-start
  201.7 4.9 collective-permute-start
  216.6 4.9 collective-permute-start
  231.6 4.9 collective-permute-start
  246.6 4.9 collective-permute-start
  261.5 4.9 collective-permute-start
  276.5 4.9 collective-permute-start
  291.5 4.9 collective-permute-start
  306.4 4.9 collective-permute-start
  321.4 4.9 collective-permute-start
  336.4 4.9 collective-permute-start
  351.3 4.9 collective-permute-start
  366.3 4.9 collective-permute-start
  381.3 4.9 collective-permute-start
  397.0 4.9 collective-permute-start.1
  412.0 4.9 collective-permute-start.1
  427.0 4.9 collective-permute-start.1
  441.9 4.9 collective-permute-start.1
  456.9 4.9 collective-permute-start.1
  471.9 4.9 collective-permute-start.1
  486.8 4.9 collective-permute-start.1
  516.8 4.9 collective-permute-start.1
  546.7 4.9 collective-permute-start.1
  624.6 16.9 collective-permute-start.2
  653.8 28.5 %collective-permute-start.2 = (bf16[32,1024]{1,0:T(8,128)(2,1)S(1)}, bf16[32,1024]{1,0:T(8,128)(2,1)S(1)}, u32[]{:S(2)}, u32[]{:S(2)}) collective-permute-start(bf16[32,1024]{1,0:T(8,128)(2,1)S(1)} %fusion.162), channel_id=1, source_target_pairs={{0,7},{1,0},{2,1},{3,2},{4,3},{5,4},{6,5},{7,6},{8,15},{9,8},{10,9... | collective-permute-start | bytes 196616 | tf_op jit(solution)/shard_map/while/body/eval_jaxpr/ppermute | solution.py:112
  694.5 28.5 %collective-permute-start.2 = (bf16[32,1024]{1,0:T(8,128)(2,1)S(1)}, bf16[32,1024]{1,0:T(8,128)(2,1)S(1)}, u32[]{:S(2)}, u32[]{:S(2)}) collective-permute-start(bf16[32,1024]{1,0:T(8,128)(2,1)S(1)} %fusion.162), channel_id=1, source_target_pairs={{0,7},{1,0},{2,1},{3,2},{4,3},{5,4},{6,5},{7,6},{8,15},{9,8},{10,9... | collective-permute-start | bytes 196616 | tf_op jit(solution)/shard_map/while/body/eval_jaxpr/ppermute | solution.py:112
  735.3 28.5 %collective-permute-start.2 = (bf16[32,1024]{1,0:T(8,128)(2,1)S(1)}, bf16[32,1024]{1,0:T(8,128)(2,1)S(1)}, u32[]{:S(2)}, u32[]{:S(2)}) collective-permute-start(bf16[32,1024]{1,0:T(8,128)(2,1)S(1)} %fusion.162), channel_id=1, source_target_pairs={{0,7},{1,0},{2,1},{3,2},{4,3},{5,4},{6,5},{7,6},{8,15},{9,8},{10,9... | collective-permute-start | bytes 196616 | tf_op jit(solution)/shard_map/while/body/eval_jaxpr/ppermute | solution.py:112
  776.0 28.5 %collective-permute-start.2 = (bf16[32,1024]{1,0:T(8,128)(2,1)S(1)}, bf16[32,1024]{1,0:T(8,128)(2,1)S(1)}, u32[]{:S(2)}, u32[]{:S(2)}) collective-permute-start(bf16[32,1024]{1,0:T(8,128)(2,1)S(1)} %fusion.162), channel_id=1, source_target_pairs={{0,7},{1,0},{2,1},{3,2},{4,3},{5,4},{6,5},{7,6},{8,15},{9,8},{10,9... | collective-permute-start | bytes 196616 | tf_op jit(solution)/shard_map/while/body/eval_jaxpr/ppermute | solution.py:112
  816.8 28.5 %collective-permute-start.2 = (bf16[32,1024]{1,0:T(8,128)(2,1)S(1)}, bf16[32,1024]{1,0:T(8,128)(2,1)S(1)}, u32[]{:S(2)}, u32[]{:S(2)}) collective-permute-start(bf16[32,1024]{1,0:T(8,128)(2,1)S(1)} %fusion.162), channel_id=1, source_target_pairs={{0,7},{1,0},{2,1},{3,2},{4,3},{5,4},{6,5},{7,6},{8,15},{9,8},{10,9... | collective-permute-start | bytes 196616 | tf_op jit(solution)/shard_map/while/body/eval_jaxpr/ppermute | solution.py:112
  857.5 29.4 %collective-permute-start.2 = (bf16[32,1024]{1,0:T(8,128)(2,1)S(1)}, bf16[32,1024]{1,0:T(8,128)(2,1)S(1)}, u32[]{:S(2)}, u32[]{:S(2)}) collective-permute-start(bf16[32,1024]{1,0:T(8,128)(2,1)S(1)} %fusion.162), channel_id=1, source_target_pairs={{0,7},{1,0},{2,1},{3,2},{4,3},{5,4},{6,5},{7,6},{8,15},{9,8},{10,9... | collective-permute-start | bytes 196616 | tf_op jit(solution)/shard_map/while/body/eval_jaxpr/ppermute | solution.py:112
  899.2 32.6 %collective-permute-start.2 = (bf16[32,1024]{1,0:T(8,128)(2,1)S(1)}, bf16[32,1024]{1,0:T(8,128)(2,1)S(1)}, u32[]{:S(2)}, u32[]{:S(2)}) collective-permute-start(bf16[32,1024]{1,0:T(8,128)(2,1)S(1)} %fusion.162), channel_id=1, source_target_pairs={{0,7},{1,0},{2,1},{3,2},{4,3},{5,4},{6,5},{7,6},{8,15},{9,8},{10,9... | collective-permute-start | bytes 196616 | tf_op jit(solution)/shard_map/while/body/eval_jaxpr/ppermute | solution.py:112
  944.1 28.5 %collective-permute-start.2 = (bf16[32,1024]{1,0:T(8,128)(2,1)S(1)}, bf16[32,1024]{1,0:T(8,128)(2,1)S(1)}, u32[]{:S(2)}, u32[]{:S(2)}) collective-permute-start(bf16[32,1024]{1,0:T(8,128)(2,1)S(1)} %fusion.162), channel_id=1, source_target_pairs={{0,7},{1,0},{2,1},{3,2},{4,3},{5,4},{6,5},{7,6},{8,15},{9,8},{10,9... | collective-permute-start | bytes 196616 | tf_op jit(solution)/shard_map/while/body/eval_jaxpr/ppermute | solution.py:112
  984.9 28.5 %collective-permute-start.2 = (bf16[32,1024]{1,0:T(8,128)(2,1)S(1)}, bf16[32,1024]{1,0:T(8,128)(2,1)S(1)}, u32[]{:S(2)}, u32[]{:S(2)}) collective-permute-start(bf16[32,1024]{1,0:T(8,128)(2,1)S(1)} %fusion.162), channel_id=1, source_target_pairs={{0,7},{1,0},{2,1},{3,2},{4,3},{5,4},{6,5},{7,6},{8,15},{9,8},{10,9... | collective-permute-start | bytes 196616 | tf_op jit(solution)/shard_map/while/body/eval_jaxpr/ppermute | solution.py:112
  1025.6 28.5 %collective-permute-start.2 = (bf16[32,1024]{1,0:T(8,128)(2,1)S(1)}, bf16[32,1024]{1,0:T(8,128)(2,1)S(1)}, u32[]{:S(2)}, u32[]{:S(2)}) collective-permute-start(bf16[32,1024]{1,0:T(8,128)(2,1)S(1)} %fusion.162), channel_id=1, source_target_pairs={{0,7},{1,0},{2,1},{3,2},{4,3},{5,4},{6,5},{7,6},{8,15},{9,8},{10,9... | collective-permute-start | bytes 196616 | tf_op jit(solution)/shard_map/while/body/eval_jaxpr/ppermute | solution.py:112
  1066.4 28.5 %collective-permute-start.2 = (bf16[32,1024]{1,0:T(8,128)(2,1)S(1)}, bf16[32,1024]{1,0:T(8,128)(2,1)S(1)}, u32[]{:S(2)}, u32[]{:S(2)}) collective-permute-start(bf16[32,1024]{1,0:T(8,128)(2,1)S(1)} %fusion.162), channel_id=1, source_target_pairs={{0,7},{1,0},{2,1},{3,2},{4,3},{5,4},{6,5},{7,6},{8,15},{9,8},{10,9... | collective-permute-start | bytes 196616 | tf_op jit(solution)/shard_map/while/body/eval_jaxpr/ppermute | solution.py:112
  1107.1 28.5 %collective-permute-start.2 = (bf16[32,1024]{1,0:T(8,128)(2,1)S(1)}, bf16[32,1024]{1,0:T(8,128)(2,1)S(1)}, u32[]{:S(2)}, u32[]{:S(2)}) collective-permute-start(bf16[32,1024]{1,0:T(8,128)(2,1)S(1)} %fusion.162), channel_id=1, source_target_pairs={{0,7},{1,0},{2,1},{3,2},{4,3},{5,4},{6,5},{7,6},{8,15},{9,8},{10,9... | collective-permute-start | bytes 196616 | tf_op jit(solution)/shard_map/while/body/eval_jaxpr/ppermute | solution.py:112
  1147.9 28.5 %collective-permute-start.2 = (bf16[32,1024]{1,0:T(8,128)(2,1)S(1)}, bf16[32,1024]{1,0:T(8,128)(2,1)S(1)}, u32[]{:S(2)}, u32[]{:S(2)}) collective-permute-start(bf16[32,1024]{1,0:T(8,128)(2,1)S(1)} %fusion.162), channel_id=1, source_target_pairs={{0,7},{1,0},{2,1},{3,2},{4,3},{5,4},{6,5},{7,6},{8,15},{9,8},{10,9... | collective-permute-start | bytes 196616 | tf_op jit(solution)/shard_map/while/body/eval_jaxpr/ppermute | solution.py:112
  1188.6 29.4 %collective-permute-start.2 = (bf16[32,1024]{1,0:T(8,128)(2,1)S(1)}, bf16[32,1024]{1,0:T(8,128)(2,1)S(1)}, u32[]{:S(2)}, u32[]{:S(2)}) collective-permute-start(bf16[32,1024]{1,0:T(8,128)(2,1)S(1)} %fusion.162), channel_id=1, source_target_pairs={{0,7},{1,0},{2,1},{3,2},{4,3},{5,4},{6,5},{7,6},{8,15},{9,8},{10,9... | collective-permute-start | bytes 196616 | tf_op jit(solution)/shard_map/while/body/eval_jaxpr/ppermute | solution.py:112
  1218.1 723.4 %reduce-scatter.11.cloned.1.call-start = ((), (), s32[]{:S(2)}) async-start(), calls=%async_computation.8 | async-start | bytes 17825792 | tf_op jit(solution)/shard_map/reduce_scatter | solution.py:124
  1230.7 21.9 collective-permute-start.3
  1264.9 28.5 %collective-permute-start.3 = (bf16[32,1024]{1,0:T(8,128)(2,1)S(1)}, bf16[32,1024]{1,0:T(8,128)(2,1)S(1)}, u32[]{:S(2)}, u32[]{:S(2)}) collective-permute-start(bf16[32,1024]{1,0:T(8,128)(2,1)S(1)} %fusion.175), channel_id=1, source_target_pairs={{0,7},{1,0},{2,1},{3,2},{4,3},{5,4},{6,5},{7,6},{8,15},{9,8},{10,9... | collective-permute-start | bytes 196616 | tf_op jit(solution)/shard_map/while/body/eval_jaxpr/ppermute | solution.py:112
  1305.7 28.5 %collective-permute-start.3 = (bf16[32,1024]{1,0:T(8,128)(2,1)S(1)}, bf16[32,1024]{1,0:T(8,128)(2,1)S(1)}, u32[]{:S(2)}, u32[]{:S(2)}) collective-permute-start(bf16[32,1024]{1,0:T(8,128)(2,1)S(1)} %fusion.175), channel_id=1, source_target_pairs={{0,7},{1,0},{2,1},{3,2},{4,3},{5,4},{6,5},{7,6},{8,15},{9,8},{10,9... | collective-permute-start | bytes 196616 | tf_op jit(solution)/shard_map/while/body/eval_jaxpr/ppermute | solution.py:112
  1346.5 28.5 %collective-permute-start.3 = (bf16[32,1024]{1,0:T(8,128)(2,1)S(1)}, bf16[32,1024]{1,0:T(8,128)(2,1)S(1)}, u32[]{:S(2)}, u32[]{:S(2)}) collective-permute-start(bf16[32,1024]{1,0:T(8,128)(2,1)S(1)} %fusion.175), channel_id=1, source_target_pairs={{0,7},{1,0},{2,1},{3,2},{4,3},{5,4},{6,5},{7,6},{8,15},{9,8},{10,9... | collective-permute-start | bytes 196616 | tf_op jit(solution)/shard_map/while/body/eval_jaxpr/ppermute | solution.py:112
  1387.4 28.5 %collective-permute-start.3 = (bf16[32,1024]{1,0:T(8,128)(2,1)S(1)}, bf16[32,1024]{1,0:T(8,128)(2,1)S(1)}, u32[]{:S(2)}, u32[]{:S(2)}) collective-permute-start(bf16[32,1024]{1,0:T(8,128)(2,1)S(1)} %fusion.175), channel_id=1, source_target_pairs={{0,7},{1,0},{2,1},{3,2},{4,3},{5,4},{6,5},{7,6},{8,15},{9,8},{10,9... | collective-permute-start | bytes 196616 | tf_op jit(solution)/shard_map/while/body/eval_jaxpr/ppermute | solution.py:112
  1428.2 28.5 %collective-permute-start.3 = (bf16[32,1024]{1,0:T(8,128)(2,1)S(1)}, bf16[32,1024]{1,0:T(8,128)(2,1)S(1)}, u32[]{:S(2)}, u32[]{:S(2)}) collective-permute-start(bf16[32,1024]{1,0:T(8,128)(2,1)S(1)} %fusion.175), channel_id=1, source_target_pairs={{0,7},{1,0},{2,1},{3,2},{4,3},{5,4},{6,5},{7,6},{8,15},{9,8},{10,9... | collective-permute-start | bytes 196616 | tf_op jit(solution)/shard_map/while/body/eval_jaxpr/ppermute | solution.py:112
  1469.0 28.5 %collective-permute-start.3 = (bf16[32,1024]{1,0:T(8,128)(2,1)S(1)}, bf16[32,1024]{1,0:T(8,128)(2,1)S(1)}, u32[]{:S(2)}, u32[]{:S(2)}) collective-permute-start(bf16[32,1024]{1,0:T(8,128)(2,1)S(1)} %fusion.175), channel_id=1, source_target_pairs={{0,7},{1,0},{2,1},{3,2},{4,3},{5,4},{6,5},{7,6},{8,15},{9,8},{10,9... | collective-permute-start | bytes 196616 | tf_op jit(solution)/shard_map/while/body/eval_jaxpr/ppermute | solution.py:112
  1509.8 29.4 %collective-permute-start.3 = (bf16[32,1024]{1,0:T(8,128)(2,1)S(1)}, bf16[32,1024]{1,0:T(8,128)(2,1)S(1)}, u32[]{:S(2)}, u32[]{:S(2)}) collective-permute-start(bf16[32,1024]{1,0:T(8,128)(2,1)S(1)} %fusion.175), channel_id=1, source_target_pairs={{0,7},{1,0},{2,1},{3,2},{4,3},{5,4},{6,5},{7,6},{8,15},{9,8},{10,9... | collective-permute-start | bytes 196616 | tf_op jit(solution)/shard_map/while/body/eval_jaxpr/ppermute | solution.py:112
  1551.6 32.6 %collective-permute-start.3 = (bf16[32,1024]{1,0:T(8,128)(2,1)S(1)}, bf16[32,1024]{1,0:T(8,128)(2,1)S(1)}, u32[]{:S(2)}, u32[]{:S(2)}) collective-permute-start(bf16[32,1024]{1,0:T(8,128)(2,1)S(1)} %fusion.175), channel_id=1, source_target_pairs={{0,7},{1,0},{2,1},{3,2},{4,3},{5,4},{6,5},{7,6},{8,15},{9,8},{10,9... | collective-permute-start | bytes 196616 | tf_op jit(solution)/shard_map/while/body/eval_jaxpr/ppermute | solution.py:112
  1596.5 28.5 %collective-permute-start.3 = (bf16[32,1024]{1,0:T(8,128)(2,1)S(1)}, bf16[32,1024]{1,0:T(8,128)(2,1)S(1)}, u32[]{:S(2)}, u32[]{:S(2)}) collective-permute-start(bf16[32,1024]{1,0:T(8,128)(2,1)S(1)} %fusion.175), channel_id=1, source_target_pairs={{0,7},{1,0},{2,1},{3,2},{4,3},{5,4},{6,5},{7,6},{8,15},{9,8},{10,9... | collective-permute-start | bytes 196616 | tf_op jit(solution)/shard_map/while/body/eval_jaxpr/ppermute | solution.py:112
  1637.4 28.5 %collective-permute-start.3 = (bf16[32,1024]{1,0:T(8,128)(2,1)S(1)}, bf16[32,1024]{1,0:T(8,128)(2,1)S(1)}, u32[]{:S(2)}, u32[]{:S(2)}) collective-permute-start(bf16[32,1024]{1,0:T(8,128)(2,1)S(1)} %fusion.175), channel_id=1, source_target_pairs={{0,7},{1,0},{2,1},{3,2},{4,3},{5,4},{6,5},{7,6},{8,15},{9,8},{10,9... | collective-permute-start | bytes 196616 | tf_op jit(solution)/shard_map/while/body/eval_jaxpr/ppermute | solution.py:112
  1678.3 28.5 %collective-permute-start.3 = (bf16[32,1024]{1,0:T(8,128)(2,1)S(1)}, bf16[32,1024]{1,0:T(8,128)(2,1)S(1)}, u32[]{:S(2)}, u32[]{:S(2)}) collective-permute-start(bf16[32,1024]{1,0:T(8,128)(2,1)S(1)} %fusion.175), channel_id=1, source_target_pairs={{0,7},{1,0},{2,1},{3,2},{4,3},{5,4},{6,5},{7,6},{8,15},{9,8},{10,9... | collective-permute-start | bytes 196616 | tf_op jit(solution)/shard_map/while/body/eval_jaxpr/ppermute | solution.py:112
  1719.1 28.5 %collective-permute-start.3 = (bf16[32,1024]{1,0:T(8,128)(2,1)S(1)}, bf16[32,1024]{1,0:T(8,128)(2,1)S(1)}, u32[]{:S(2)}, u32[]{:S(2)}) collective-permute-start(bf16[32,1024]{1,0:T(8,128)(2,1)S(1)} %fusion.175), channel_id=1, source_target_pairs={{0,7},{1,0},{2,1},{3,2},{4,3},{5,4},{6,5},{7,6},{8,15},{9,8},{10,9... | collective-permute-start | bytes 196616 | tf_op jit(solution)/shard_map/while/body/eval_jaxpr/ppermute | solution.py:112
  1759.9 28.5 %collective-permute-start.3 = (bf16[32,1024]{1,0:T(8,128)(2,1)S(1)}, bf16[32,1024]{1,0:T(8,128)(2,1)S(1)}, u32[]{:S(2)}, u32[]{:S(2)}) collective-permute-start(bf16[32,1024]{1,0:T(8,128)(2,1)S(1)} %fusion.175), channel_id=1, source_target_pairs={{0,7},{1,0},{2,1},{3,2},{4,3},{5,4},{6,5},{7,6},{8,15},{9,8},{10,9... | collective-permute-start | bytes 196616 | tf_op jit(solution)/shard_map/while/body/eval_jaxpr/ppermute | solution.py:112
  1800.7 28.5 %collective-permute-start.3 = (bf16[32,1024]{1,0:T(8,128)(2,1)S(1)}, bf16[32,1024]{1,0:T(8,128)(2,1)S(1)}, u32[]{:S(2)}, u32[]{:S(2)}) collective-permute-start(bf16[32,1024]{1,0:T(8,128)(2,1)S(1)} %fusion.175), channel_id=1, source_target_pairs={{0,7},{1,0},{2,1},{3,2},{4,3},{5,4},{6,5},{7,6},{8,15},{9,8},{10,9... | collective-permute-start | bytes 196616 | tf_op jit(solution)/shard_map/while/body/eval_jaxpr/ppermute | solution.py:112
  1829.3 225.8 %reduce-scatter.17.cloned.1.call-start = ((), (), s32[]{:S(2)}) async-start(), calls=%async_computation.11 | async-start | bytes 17825792 | tf_op jit(solution)/shard_map/reduce_scatter | solution.py:125
  1830.1 338.6 %reduce-scatter.15.cloned.1.call-start = ((), (), s32[]{:S(2)}) async-start(), calls=%async_computation.10 | async-start | bytes 17825792 | tf_op jit(solution)/shard_map/reduce_scatter | solution.py:125
  1830.8 371.6 %reduce-scatter.7.cloned.1.call-start = ((), (), s32[]{:S(2)}) async-start(), calls=%async_computation.6 | async-start | bytes 589824 | tf_op jit(solution)/shard_map/reduce_scatter | solution.py:86
  1832.0 403.3 %reduce-scatter.9.cloned.1.call-start = ((), (), s32[]{:S(2)}) async-start(), calls=%async_computation.7 | async-start | bytes 589824 | tf_op jit(solution)/shard_map/reduce_scatter | solution.py:127
  (99 other events, 708.6 us)
Sparse Core Ops, SparseCore 0:
  10.7 78.4 all-gather.8
  91.3 70.2 all-gather.10
  164.3 75.8 all-gather.12
  242.3 70.1 all-gather.14
  1218.2 111.3 reduce-scatter.12
  1829.4 112.0 reduce-scatter.10
  1944.9 110.0 reduce-scatter.16
  2058.5 110.1 reduce-scatter.14
  2171.6 30.8 reduce-scatter.6
  2205.2 30.0 reduce-scatter.8
where the time goes:
time: 2250 us; the launch traced here: 2240 us
  matrix products  1380 us (61%)
  waiting for transfers between devices  645 us (29%)
  loops' own time  84.4 us (4%)
  local copies, waits for them, and re-layouts  62.2 us (3%)
  blocking collectives  26.6 us (1%)
    dot_general x30, matrix products, layer_bwd(): lax.dot_general(h_in, d_pre, (((0,), (0,)), ((), ())), preferred_element_...  407 us
    dot_general x30, matrix products, layer_bwd(): lax.dot_general(act_val, g_out, (((0,), (0,)), ((), ())), preferred_eleme...  405 us
    dot_general x30, matrix products, layer_fwd(): branch = jnp.dot(act_val, w_two, preferred_element_type=jnp.float32)  263 us
    reduce_scatter x2, waiting for transfers between devices, device_step(): lax.psum_scatter(jnp.stack(end_state[3]), 'inner', scatter_dimension=1, t...  224 us
    dot_general x30, matrix products, layer_bwd(): pre_act = jnp.dot(h_in, w_one, preferred_element_type=jnp.float32)  153 us
    ppermute x30, waiting for transfers between devices, fwd_tick(): sent_act = lax.ppermute(h_act, 'stage', fwd_perm)  124 us
    reduce_scatter x2, waiting for transfers between devices, device_step(): lax.psum_scatter(jnp.stack(end_state[2]), 'inner', scatter_dimension=2, t...  109 us
    dot_general x30, matrix products, layer_bwd(): lax.dot_general(g_out, w_two, (((1,), (1,)), ((), ())), preferred_element...  77.9 us
  transfers between devices with their start and end apart: 70, of which 37 were waited for; matrix products, arithmetic and copies ran while one was open for 50% of the time, Pallas kernels for 0%

commit v1 on v0

v1 whole, which is shorter than its diff:
```python
import functools

import jax
import jax.numpy as jnp
from jax import lax
from jax.experimental import pallas as pl
from jax.experimental.pallas import tpu as pltpu
from jax.sharding import PartitionSpec as P

MESH = pl.DeviceIdType.MESH
NT = (((1,), (1,)), ((), ()))
TN = (((0,), (0,)), ((), ()))
SIDE = 4
CHUNKS = 2
F32 = jnp.float32
BF16 = jnp.bfloat16


def gelu_parts(pre_act):
    normal_cdf = 0.5 * (1.0 + lax.erf(pre_act * 0.7071067811865476))
    normal_pdf = jnp.exp(-0.5 * pre_act * pre_act) * 0.3989422804014327
    return normal_cdf, normal_pdf


def remote(src, dst, send_sem, recv_sem, inner, stage):
    return pltpu.make_async_remote_copy(
        src_ref=src, dst_ref=dst, send_sem=send_sem, recv_sem=recv_sem,
        device_id={'inner': inner, 'stage': stage}, device_id_type=MESH)


class PlaneGather:
    def __init__(self, own, slot, recv_sems, send_sem, inner, stage, y_first):
        self.own, self.slot, self.recv_sems, self.send_sem = own, slot, recv_sems, send_sem
        self.inner, self.stage, self.y_first = inner, stage, y_first
        z_pos, y_pos = lax.div(inner, SIDE), lax.rem(inner, SIDE)
        self.a_pos, self.b_pos = (y_pos, z_pos) if y_first else (z_pos, y_pos)

    def block(self, a_off, b_off):
        a_pos = lax.rem(self.a_pos + a_off + SIDE, SIDE)
        b_pos = lax.rem(self.b_pos + b_off + SIDE, SIDE)
        return b_pos * SIDE + a_pos if self.y_first else a_pos * SIDE + b_pos

    def send(self, block, half, a_off, b_off, sem_idx, own=False):
        src = self.own(half) if own else self.slot(block, half)
        remote(src, self.slot(block, half), self.send_sem, self.recv_sems(sem_idx),
               self.block(a_off, b_off), self.stage).start()

    def wait(self, block, half, sem_idx):
        ref = self.slot(block, half)
        remote(ref, ref, self.send_sem, self.recv_sems(sem_idx), self.inner, self.stage).wait_recv()

    def step_own(self):
        self.send(self.inner, None, 1, 0, 0, own=True)
        self.send(self.inner, None, -1, 0, 1, own=True)

    def step_own_across(self):
        self.send(self.inner, None, 0, 1, 4, own=True)
        self.send(self.inner, None, 0, -1, 5, own=True)

    def step_near(self):
        for side, half in ((-1, 0), (1, 1)):
            block = self.block(side, 0)
            self.wait(block, None, half)
            self.send(block, half, -side, 0, 2 + half)
            for toward in (1, -1):
                self.send(block, None, 0, toward, 4 + 4 * (1 + half) + (0 if toward == 1 else 1))

    def step_far(self):
        block = self.block(2, 0)
        self.wait(block, 0, 2)
        self.wait(block, 1, 3)
        for toward in (1, -1):
            self.send(block, None, 0, toward, 4 + 12 + (0 if toward == 1 else 1))

    def step_relay(self):
        for role, a_off in enumerate((0, -1, 1, 2)):
            for side, half in ((-1, 0), (1, 1)):
                block = self.block(a_off, side)
                self.wait(block, None, 4 + 4 * role + half)
                self.send(block, half, 0, -side, 4 + 4 * role + 2 + half)

    def step_last(self):
        for role, a_off in enumerate((0, -1, 1, 2)):
            block = self.block(a_off, 2)
            for half in (0, 1):
                self.wait(block, half, 4 + 4 * role + 2 + half)

    def step_sent(self, many):
        remote(many, many, self.send_sem, self.recv_sems(0), self.inner, self.stage).wait_send()


class Pair:
    def __init__(self, *parts):
        self.parts = parts

    def __getattr__(self, name):
        def call():
            for part in self.parts:
                getattr(part, name)()
        return call


def main_kernel(n_stage, x_ref, g_ref, wu_ref, wd_ref, y_ref, dx_ref, h_all, g_all,
                w1, w2, zb, act, hb, gb, ho, go,
                load_sem, keep_sem, ag_recv, ag_send, xr, xs, gr, gs, fr, fs, br, bs, yr, ys, dr, ds):
    inner = lax.axis_index('inner')
    stage = lax.axis_index('stage')
    first, last = stage == 0, stage == n_stage - 1
    n_inner = SIDE * SIDE
    n_blk, d_model, f_blk = w1.shape[1:]
    tok = x_ref.shape[1]
    rows = hb.shape[2]
    per_chunk = rows // tok
    half_w1, half_w2 = d_model // 2, f_blk // 2
    half_rows = rows // 2

    loads = []
    for v in range(2):
        loads.append(pltpu.make_async_copy(wu_ref.at[v, 0], w1.at[v, inner], load_sem.at[v, 0]))
        loads.append(pltpu.make_async_copy(wd_ref.at[v, 0], w2.at[v, inner], load_sem.at[v, 1]))
    for load in loads:
        load.start()

    barrier = pltpu.get_barrier_semaphore()
    z_pos, y_pos = lax.div(inner, SIDE), lax.rem(inner, SIDE)
    for off in (1, SIDE - 1):
        for peer in (z_pos * SIDE + lax.rem(y_pos + off, SIDE), lax.rem(z_pos + off, SIDE) * SIDE + y_pos):
            pl.semaphore_signal(barrier, inc=1, device_id={'inner': peer, 'stage': stage}, device_id_type=MESH)
    for off in range(1, n_stage):
        peer = lax.rem(stage + off, n_stage)
        pl.semaphore_signal(barrier, inc=1, device_id={'inner': inner, 'stage': peer}, device_id_type=MESH)
    pl.semaphore_wait(barrier, 4 + n_stage - 1)

    def rows_of(micro):
        return pl.ds(pl.multiple_of(lax.rem(micro, per_chunk) * tok, tok), tok)

    def w_slot(buf, v, half_size):
        def slot(block, half):
            ref = buf.at[v, block]
            return ref if half is None else ref.at[pl.ds(half * half_size, half_size)]
        return slot

    def make_w(v):
        parts = []
        for colour, (buf, half_size) in enumerate(((w1, half_w1), (w2, half_w2))):
            slot = w_slot(buf, v, half_size)
            parts.append(PlaneGather(
                functools.partial(slot, inner), slot, lambda k, u=v, c=colour: ag_recv.at[u, c, k],
                ag_send.at[v, colour], inner, stage, colour == 0))
        return Pair(*parts)

    def make_act(unit, buf, out, v):
        parts = []
        for colour in range(2):
            def own(half, colour=colour):
                ref = buf.at[v, colour]
                return ref if half is None else ref.at[pl.ds(half * half_rows, half_rows)]

            def slot(block, half, colour=colour):
                if half is None:
                    return out.at[v, block, pl.ds(colour * rows, rows)]
                return out.at[v, block, pl.ds(colour * rows + half * half_rows, half_rows)]

            parts.append(PlaneGather(own, slot, lambda k, u=unit, c=colour: ag_recv.at[u, c, k],
                                     ag_send.at[unit, colour], inner, stage, colour == 0))
        return Pair(*parts)

    weights = [make_w(0), make_w(1)]
    acts = [make_act(2, hb, h_all, 0), make_act(3, hb, h_all, 1), make_act(4, gb, g_all, 1), make_act(5, gb, g_all, 0)]

    for v in range(2):
        for load in loads[2 * v:2 * v + 2]:
            load.wait()
        if v == 0:
            weights[0].step_own()
            weights[0].step_own_across()

    chunk = lax.div(stage, per_chunk)
    x_dst = hb.at[0, chunk, rows_of(stage)]
    g_dst = gb.at[1, chunk, rows_of(stage)]

    @pl.when(first)
    def _():
        pltpu.make_async_copy(x_ref.at[0], x_dst, xr.at[stage]).start()

    @pl.when(jnp.logical_not(first))
    def _():
        remote(x_ref.at[0], x_dst, xs.at[0], xr.at[stage], inner, 0).start()

    @pl.when(last)
    def _():
        pltpu.make_async_copy(g_ref.at[0], g_dst, gr.at[stage]).start()

    @pl.when(jnp.logical_not(last))
    def _():
        remote(g_ref.at[0], g_dst, gs.at[0], gr.at[stage], inner, n_stage - 1).start()

    weights[0].step_near()
    weights[0].step_far()
    weights[1].step_own()
    weights[1].step_own_across()
    weights[0].step_relay()
    weights[1].step_near()
    weights[1].step_far()
    weights[0].step_last()

    def wait_in(buf, v, m, ready, micro_ready, from_tokens):
        @pl.when(from_tokens)
        def _():
            for k in range(per_chunk):
                micro = m * per_chunk + k
                ref = buf.at[v, m, pl.ds(k * tok, tok)]
                remote(ref, ref, xs.at[0], micro_ready.at[micro], inner, stage).wait_recv()

        @pl.when(jnp.logical_not(from_tokens))
        def _():
            ref = buf.at[v, m]
            remote(ref, ref, xs.at[0], ready.at[v, m], inner, stage).wait_recv()

    def give_out(buf, v, m, out_ref, sends, recv):
        for k in range(per_chunk):
            micro = m * per_chunk + k
            src = buf.at[v, m, pl.ds(k * tok, tok)]

            @pl.when(micro == stage)
            def _():
                pltpu.make_async_copy(src, out_ref.at[0], recv.at[0]).start()

            @pl.when(micro != stage)
            def _():
                remote(src, out_ref.at[0], sends.at[micro], recv.at[0], inner, micro).start()

    def forward(v, m):
        wait_in(hb, v, m, fr, xr, first & (v == 0))
        h_in = hb[v, m]
        for blk in range(n_blk):
            cols = slice(blk * f_blk, (blk + 1) * f_blk)
            pre_act = jnp.dot(h_in, w1[v, blk], preferred_element_type=F32)
            zb[v, m, :, cols] = pre_act
            normal_cdf = 0.5 * (1.0 + lax.erf(pre_act * 0.7071067811865476))
            act[:, cols] = (pre_act * normal_cdf).astype(BF16)
        branch = jnp.dot(act[...], w2[v].reshape(n_blk * f_blk, d_model), preferred_element_type=F32)
        ho[v, m] = (h_in.astype(F32) + branch).astype(BF16)
        done = last & (v == 1)

        @pl.when(done)
        def _():
            give_out(ho, v, m, y_ref, ys, yr)

        @pl.when(jnp.logical_not(done))
        def _():
            v_to = v + last.astype(jnp.int32)
            remote(ho.at[v, m], hb.at[v_to, m], fs.at[v, m], fr.at[v_to, m], inner,
                   lax.rem(stage + 1, n_stage)).start()

    def backward(v, m):
        wait_in(gb, v, m, br, gr, last & (v == 1))
        g_out = gb[v, m]
        for blk in range(n_blk):
            cols = slice(blk * f_blk, (blk + 1) * f_blk)
            d_act = lax.dot_general(g_out, w2[v, blk], NT, preferred_element_type=F32)
            pre_act = zb[v, m, :, cols]
            normal_cdf, normal_pdf = gelu_parts(pre_act)
            act[:, cols] = (d_act * (normal_cdf + pre_act * normal_pdf)).astype(BF16)
        back = None
        for blk in range(n_blk):
            cols = slice(blk * f_blk, (blk + 1) * f_blk)
            term = lax.dot_general(act[:, cols], w1[v, blk], NT, preferred_element_type=F32)
            back = term if back is None else back + term
        go[v, m] = (g_out.astype(F32) + back).astype(BF16)
        done = first & (v == 0)

        @pl.when(done)
        def _():
            give_out(go, v, m, dx_ref, ds, dr)

        @pl.when(jnp.logical_not(done))
        def _():
            v_to = v - first.astype(jnp.int32)
            remote(go.at[v, m], gb.at[v_to, m], bs.at[v, m], br.at[v_to, m], inner,
                   lax.rem(stage + n_stage - 1, n_stage)).start()

    tail = CHUNKS - 1
    starts = (n_stage,
              jnp.maximum(n_stage + 6, n_stage + stage + tail),
              jnp.maximum(2 * n_stage + 4, 3 * n_stage - 1 - stage + tail),
              jnp.maximum(3 * n_stage + 2, 4 * n_stage - 1 - stage + tail))
    offsets = (('step_own', 0), ('step_own_across', 0), ('step_near', 1), ('step_far', 2), ('step_relay', 4))

    def tick(t, carry):
        ahead = t - stage
        f_pos = jnp.maximum(ahead, 0)
        f_v, f_m = lax.div(f_pos, n_stage), lax.rem(f_pos, n_stage)
        f_on = (ahead >= 0) & (f_v < 2) & (f_m < CHUNKS)
        behind = t - (3 * n_stage - 1) + stage
        b_pos = jnp.maximum(behind, 0)
        b_k, b_m = lax.div(b_pos, n_stage), lax.rem(b_pos, n_stage)
        b_on = (behind >= 0) & (b_k < 2) & (b_m < CHUNKS)

        @pl.when(t == n_stage)
        def _():
            weights[1].step_relay()

        @pl.when(f_on & (f_v == 1) & (f_m == 0))
        def _():
            weights[1].step_last()

        @pl.when(f_on)
        def _():
            forward(f_v, f_m)

        @pl.when(b_on)
        def _():
            backward(1 - b_k, b_m)

        for unit, start in zip(acts, starts):
            for name, off in offsets:
                @pl.when(t == start + off)
                def _():
                    getattr(unit, name)()
        return carry

    lax.fori_loop(0, 4 * n_stage + 7, tick, 0)

    keeps = []
    for k, (buf, out) in enumerate(((hb, h_all), (gb, g_all))):
        for v in range(2):
            for m in range(CHUNKS):
                keeps.append(pltpu.make_async_copy(
                    buf.at[v, m], out.at[v, inner, pl.ds(m * rows, rows)], keep_sem.at[k, v, m]))
    for keep in keeps:
        keep.start()
    for unit in acts:
        unit.step_last()
    for keep in keeps:
        keep.wait()
    for v in range(2):
        for part, buf in zip(weights[v].parts, (w1, w2)):
            part.step_sent(buf.at[v, pl.ds(0, n_inner - 1)])
    for unit, (v, out) in zip(acts, ((0, h_all), (1, h_all), (1, g_all), (0, g_all))):
        for colour, part in enumerate(unit.parts):
            part.step_sent(out.at[v, pl.ds(0, n_inner - 1), pl.ds(colour * rows, rows)])

    def wait_sent(ref, sem):
        remote(ref, ref, sem, xr.at[0], inner, stage).wait_send()

    @pl.when(jnp.logical_not(first))
    def _():
        wait_sent(x_ref.at[0], xs.at[0])

    @pl.when(jnp.logical_not(last))
    def _():
        wait_sent(g_ref.at[0], gs.at[0])

    for v in range(2):
        for m in range(CHUNKS):
            @pl.when(jnp.logical_not(last & (v == 1)))
            def _():
                wait_sent(ho.at[v, m], fs.at[v, m])

            @pl.when(jnp.logical_not(first & (v == 0)))
            def _():
                wait_sent(go.at[v, m], bs.at[v, m])

    for micro in range(n_stage):
        @pl.when(last & (stage != micro))
        def _():
            wait_sent(ho.at[1, 0, pl.ds(0, tok)], ys.at[micro])

        @pl.when(first & (stage != micro))
        def _():
            wait_sent(go.at[0, 0, pl.ds(0, tok)], ds.at[micro])

    remote(y_ref.at[0], y_ref.at[0], xs.at[0], yr.at[0], inner, stage).wait_recv()
    remote(dx_ref.at[0], dx_ref.at[0], xs.at[0], dr.at[0], inner, stage).wait_recv()


def grad_kernel(h_ref, g_ref, wu_ref, wd_ref, du_ref, dd_ref, acc):
    step = pl.program_id(1)

    @pl.when(step == 0)
    def _():
        acc[...] = jnp.zeros_like(acc)
        dd_ref[...] = jnp.zeros_like(dd_ref)

    h_in, g_out = h_ref[0], g_ref[0]
    pre_act = jnp.dot(h_in, wu_ref[0, 0], preferred_element_type=F32)
    d_act = lax.dot_general(g_out, wd_ref[0, 0], NT, preferred_element_type=F32)
    normal_cdf, normal_pdf = gelu_parts(pre_act)
    act_val = (pre_act * normal_cdf).astype(BF16)
    d_pre = (d_act * (normal_cdf + pre_act * normal_pdf)).astype(BF16)
    acc[...] += lax.dot_general(d_pre, h_in, TN, preferred_element_type=F32)
    dd_ref[0, 0] += lax.dot_general(act_val, g_out, TN, preferred_element_type=F32)

    @pl.when(step == pl.num_programs(1) - 1)
    def _():
        du_ref[0, 0] = acc[...].T


def solution(mesh):
    n_stage = mesh.shape['stage']
    n_inner = mesh.shape['inner']
    tok_spec = P(('data', 'stage', 'inner'))
    up_spec = P(None, ('data', 'stage'), None, 'inner')
    down_spec = P(None, ('data', 'stage'), 'inner', None)

    def device_step(x_loc, g_loc, w_up, w_down):
        tok, d_model = x_loc.shape[1:]
        f_blk = w_up.shape[3]
        rows = n_stage * tok // CHUNKS
        lane = n_stage * tok
        f_full = n_inner * f_blk
        any_spec = pl.BlockSpec(memory_space=pl.ANY)
        dma = pltpu.SemaphoreType.DMA
        y_loc, dx_loc, h_all, g_all = pl.pallas_call(
            functools.partial(main_kernel, n_stage),
            name='stack',
            out_shape=(jax.ShapeDtypeStruct(x_loc.shape, BF16), jax.ShapeDtypeStruct(x_loc.shape, BF16),
                       jax.ShapeDtypeStruct((2, n_inner, lane, d_model), BF16),
                       jax.ShapeDtypeStruct((2, n_inner, lane, d_model), BF16)),
            in_specs=[any_spec] * 4,
            out_specs=(any_spec,) * 4,
            scratch_shapes=[
                pltpu.VMEM((2, n_inner, d_model, f_blk), BF16),
                pltpu.VMEM((2, n_inner, f_blk, d_model), BF16),
                pltpu.VMEM((2, CHUNKS, rows, f_full), F32),
                pltpu.VMEM((rows, f_full), BF16),
                pltpu.VMEM((2, CHUNKS, rows, d_model), BF16),
                pltpu.VMEM((2, CHUNKS, rows, d_model), BF16),
                pltpu.VMEM((2, CHUNKS, rows, d_model), BF16),
                pltpu.VMEM((2, CHUNKS, rows, d_model), BF16),
                dma((2, 2)), dma((2, 2, CHUNKS)), dma((6, 2, 20)), dma((6, 2)),
                dma((n_stage,)), dma((1,)), dma((n_stage,)), dma((1,)),
                dma((2, CHUNKS)), dma((2, CHUNKS)), dma((2, CHUNKS)), dma((2, CHUNKS)),
                dma((1,)), dma((n_stage,)), dma((1,)), dma((n_stage,)),
            ],
            compiler_params=pltpu.CompilerParams(
                collective_id=0, has_side_effects=True, vmem_limit_bytes=60 << 20),
        )(x_loc, g_loc, w_up, w_down)

        tokens = n_inner * lane
        blk = min(512, tokens)
        h_all = h_all.reshape(2, tokens, d_model)
        g_all = g_all.reshape(2, tokens, d_model)
        dw_up, dw_down = pl.pallas_call(
            grad_kernel,
            name='grads',
            grid=(2, tokens // blk),
            out_shape=(jax.ShapeDtypeStruct(w_up.shape, F32), jax.ShapeDtypeStruct(w_down.shape, F32)),
            in_specs=[pl.BlockSpec((1, blk, d_model), lambda v, t: (v, t, 0)),
                      pl.BlockSpec((1, blk, d_model), lambda v, t: (v, t, 0)),
                      pl.BlockSpec((1, 1, d_model, f_blk), lambda v, t: (v, 0, 0, 0)),
                      pl.BlockSpec((1, 1, f_blk, d_model), lambda v, t: (v, 0, 0, 0))],
            out_specs=(pl.BlockSpec((1, 1, d_model, f_blk), lambda v, t: (v, 0, 0, 0)),
                       pl.BlockSpec((1, 1, f_blk, d_model), lambda v, t: (v, 0, 0, 0))),
            scratch_shapes=[pltpu.VMEM((f_blk, d_model), F32)],
            compiler_params=pltpu.CompilerParams(
                dimension_semantics=('arbitrary', 'arbitrary'), vmem_limit_bytes=40 << 20),
        )(h_all, g_all, w_up, w_down)
        return y_loc, dx_loc, dw_up, dw_down

    return jax.shard_map(device_step, mesh=mesh, in_specs=(tok_spec, tok_spec, up_spec, down_spec),
                         out_specs=(tok_spec, tok_spec, up_spec, down_spec), check_vma=False)
```

time: 2250 us -> 479 us (0.21)
  matrix products: 1380 us -> 0 us
  waiting for transfers between devices: 645 us -> 0 us
  Pallas kernels: 0 us -> 473 us
  loops' own time: 84.4 us -> 0 us
  local copies, waits for them, and re-layouts: 62.2 us -> 3.71 us
  blocking collectives: 26.6 us -> 0 us
    dot_general x180 -> x0, matrix products: 1380 us -> none  [the longest x30 407 us: layer_bwd(): lax.dot_general(h_in, d_pre, (((0,), (0,)), ((), ())), preferred_element_...]
    pallas_call x0 -> x2, Pallas kernels: none -> 473 us  [the longest x1 444 us: device_step(): pl.pallas_call(functools.partial(main_kernel, n_stage), name='stack', out...]
    reduce_scatter x6 -> x0, waiting for transfers between devices: 396 us -> none  [the longest x2 224 us: device_step(): lax.psum_scatter(jnp.stack(end_state[3]), 'inner', scatter_dimension=1, t...]
    ppermute x60 -> x0, waiting for transfers between devices: 124 us -> none  [the longest x30 124 us: fwd_tick(): sent_act = lax.ppermute(h_act, 'stage', fwd_perm)]
    all_gather x4 -> x0, waiting for transfers between devices: 122 us -> none  [the longest x2 72.4 us: device_step(): down_full = lax.all_gather(w_down[virt_idx], 'inner', axis=1, tiled=True)]
    another operation x4 -> x0, loops' own time: 84.4 us -> none  [the longest x2 42.6 us: device_step(): lax.scan(bwd_tick, (grad_buf, act_zero, acc_init_one, acc_init_two), tick...]
    dynamic_slice x150 -> x0, local copies, waits for them, and re-layouts: 36.1 us -> none  [the longest x60 35.2 us: device_step(): end_state = lax.scan(fwd_tick, (act_buf, act_zero, saved_init), tick_ids)[0]]
    all_gather x2 -> x0, blocking collectives: 26.6 us -> none  [the longest x1 13.5 us: device_step(): x_col = lax.all_gather(x_loc, 'stage', axis=0, tiled=True)]
  transfers between devices with their start and end apart: 70 -> 0, of which waited for: 37 -> 0; matrix products, arithmetic and copies ran while one was open for 50% -> 0% of each run, Pallas kernels for 0% -> 0%
where the time goes in v1:
time: 479 us; the launch traced here: 477 us
  Pallas kernels  473 us (99%)
    pallas_call x1, Pallas kernels, device_step(): pl.pallas_call(functools.partial(main_kernel, n_stage), name='stack', out...  444 us
    pallas_call x1, Pallas kernels, device_step(): pl.pallas_call(grad_kernel, name='grads', grid=(2, tokens // blk), out_sh...  28.9 us

profile of v1, /device:TPU:8, one launch (start us, length us, event | category | flops | bytes accessed | tf_op | source)
XLA Modules:
  0.0 477.2 jit_solution(9117373994462266724)
XLA Ops:
  0.6 443.9 %stack.1 = (bf16[1,32,1024]{2,1,0:T(8,128)(2,1)}, bf16[1,32,1024]{2,1,0:T(8,128)(2,1)}, bf16[2,16,256,1024]{3,2,1,0:T(8,128)(2,1)}, bf16[2,16,256,1024]{3,2,1,0:T(8,128)(2,1)}) custom-call(bf16[1,32,1024]{2,1,0:T(8,128)(2,1)} %x_ref.1, bf16[1,32,1024]{2,1,0:T(8,128)(2,1)} %g_ref.1, bf16[2,1,1024,256]{3,2,1,0:T(8,128)(2,1)} %wu_ref.3, ...), custom_call_target="tpu_custom_call" | custom-call | tf_op jit(solution)/shard_map/stack/pallas_call | solution.py:415
  444.5 0.0 copy-start
  444.5 1.2 copy-done
  445.8 0.0 copy-start.1
  445.8 1.2 copy-done.1
  447.0 0.0 copy-start.3
  447.0 0.0 copy-start.2
  447.0 28.9 %grads.1 = (f32[2,1,1024,256]{3,2,1,0:T(8,128)}, f32[2,1,256,1024]{3,2,1,0:T(8,128)}) custom-call(bf16[2,4096,1024]{2,1,0:T(8,128)(2,1)} %bitcast.2, bf16[2,4096,1024]{2,1,0:T(8,128)(2,1)} %bitcast.3, bf16[2,1,1024,256]{3,2,1,0:T(8,128)(2,1)S(1)} %copy-done, bf16[2,1,256,1024]{3,2,1,0:T(8,128)(2,1)S(1)} %copy-done.1), custom_call_target="tpu_custom_call" | custom-call | tf_op jit(solution)/shard_map/grads/pallas_call | solution.py:445
  475.9 0.0 copy-done.3
  475.9 0.6 copy.10
  476.6 0.0 copy-done.2
  476.6 0.6 copy.11
Async XLA Ops:
  444.5 1.2 copy-start
  445.8 1.2 copy-start.1
  447.0 28.9 %copy-start.3 = (bf16[1,32,1024]{2,1,0:T(8,128)(2,1)S(1)}, bf16[1,32,1024]{2,1,0:T(8,128)(2,1)}, u32[]{:S(2)}) copy-start(bf16[1,32,1024]{2,1,0:T(8,128)(2,1)} %get-tuple-element.20) | copy-start | bytes 196612
  447.0 29.6 %copy-start.2 = (bf16[1,32,1024]{2,1,0:T(8,128)(2,1)S(1)}, bf16[1,32,1024]{2,1,0:T(8,128)(2,1)}, u32[]{:S(2)}) copy-start(bf16[1,32,1024]{2,1,0:T(8,128)(2,1)} %get-tuple-element.21) | copy-start | bytes 196612

commit v2 on v1

--- a/solution.py
+++ b/solution.py
@@ -107,17 +107,20 @@
     stage = lax.axis_index('stage')
     first, last = stage == 0, stage == n_stage - 1
     n_inner = SIDE * SIDE
-    n_blk, d_model, f_blk = w1.shape[1:]
+    n_blk, n_tile, f_blk = w1.shape[1:4]
+    d_model = n_tile * f_blk
     tok = x_ref.shape[1]
     rows = hb.shape[2]
     per_chunk = rows // tok
-    half_w1, half_w2 = d_model // 2, f_blk // 2
+    half_tiles = n_tile // 2
     half_rows = rows // 2
 
     loads = []
     for v in range(2):
-        loads.append(pltpu.make_async_copy(wu_ref.at[v, 0], w1.at[v, inner], load_sem.at[v, 0]))
-        loads.append(pltpu.make_async_copy(wd_ref.at[v, 0], w2.at[v, inner], load_sem.at[v, 1]))
+        for k in range(n_tile):
+            part = pl.ds(k * f_blk, f_blk)
+            loads.append(pltpu.make_async_copy(wu_ref.at[v, 0, part], w1.at[v, inner, k], load_sem.at[v, 0, k]))
+            loads.append(pltpu.make_async_copy(wd_ref.at[v, 0, :, part], w2.at[v, inner, k], load_sem.at[v, 1, k]))
     for load in loads:
         load.start()
 
@@ -142,7 +145,7 @@
 
     def make_w(v):
         parts = []
-        for colour, (buf, half_size) in enumerate(((w1, half_w1), (w2, half_w2))):
+        for colour, (buf, half_size) in enumerate(((w1, half_tiles), (w2, half_tiles))):
             slot = w_slot(buf, v, half_size)
             parts.append(PlaneGather(
                 functools.partial(slot, inner), slot, lambda k, u=v, c=colour: ag_recv.at[u, c, k],
@@ -169,7 +172,7 @@
     acts = [make_act(2, hb, h_all, 0), make_act(3, hb, h_all, 1), make_act(4, gb, g_all, 1), make_act(5, gb, g_all, 0)]
 
     for v in range(2):
-        for load in loads[2 * v:2 * v + 2]:
+        for load in loads[2 * n_tile * v:2 * n_tile * (v + 1)]:
             load.wait()
         if v == 0:
             weights[0].step_own()
@@ -201,7 +204,6 @@
     weights[1].step_own_across()
     weights[0].step_relay()
     weights[1].step_near()
-    weights[1].step_far()
     weights[0].step_last()
 
     def wait_in(buf, v, m, ready, micro_ready, from_tokens):
@@ -235,12 +237,14 @@
         h_in = hb[v, m]
         for blk in range(n_blk):
             cols = slice(blk * f_blk, (blk + 1) * f_blk)
-            pre_act = jnp.dot(h_in, w1[v, blk], preferred_element_type=F32)
+            pre_act = jnp.dot(h_in, w1[v, blk].reshape(d_model, f_blk), preferred_element_type=F32)
             zb[v, m, :, cols] = pre_act
             normal_cdf = 0.5 * (1.0 + lax.erf(pre_act * 0.7071067811865476))
             act[:, cols] = (pre_act * normal_cdf).astype(BF16)
-        branch = jnp.dot(act[...], w2[v].reshape(n_blk * f_blk, d_model), preferred_element_type=F32)
-        ho[v, m] = (h_in.astype(F32) + branch).astype(BF16)
+        for k in range(n_tile):
+            cols = slice(k * f_blk, (k + 1) * f_blk)
+            branch = jnp.dot(act[...], w2[v, :, k].reshape(n_blk * f_blk, f_blk), preferred_element_type=F32)
+            ho[v, m, :, cols] = (hb[v, m, :, cols].astype(F32) + branch).astype(BF16)
         done = last & (v == 1)
 
         @pl.when(done)
@@ -252,22 +256,35 @@
             v_to = v + last.astype(jnp.int32)
             remote(ho.at[v, m], hb.at[v_to, m], fs.at[v, m], fr.at[v_to, m], inner,
                    lax.rem(stage + 1, n_stage)).start()
+
+    def transpose(v):
+        for u in range(2):
+            @pl.when(v == u)
+            def _():
+                for part, buf in zip(weights[u].parts, (w1, w2)):
+                    part.step_sent(buf.at[u, pl.ds(0, n_inner - 1)])
+
+        def tiles(blk, carry):
+            for buf in (w2, w1):
+                for k in range(n_tile):
+                    buf[v, blk, k] = buf[v, blk, k].T
+            return carry
+
+        lax.fori_loop(0, n_blk, tiles, 0)
 
     def backward(v, m):
         wait_in(gb, v, m, br, gr, last & (v == 1))
         g_out = gb[v, m]
         for blk in range(n_blk):
             cols = slice(blk * f_blk, (blk + 1) * f_blk)
-            d_act = lax.dot_general(g_out, w2[v, blk], NT, preferred_element_type=F32)
+            d_act = jnp.dot(g_out, w2[v, blk].reshape(d_model, f_blk), preferred_element_type=F32)
             pre_act = zb[v, m, :, cols]
             normal_cdf, normal_pdf = gelu_parts(pre_act)
             act[:, cols] = (d_act * (normal_cdf + pre_act * normal_pdf)).astype(BF16)
-        back = None
-        for blk in range(n_blk):
-            cols = slice(blk * f_blk, (blk + 1) * f_blk)
-            term = lax.dot_general(act[:, cols], w1[v, blk], NT, preferred_element_type=F32)
-            back = term if back is None else back + term
-        go[v, m] = (g_out.astype(F32) + back).astype(BF16)
+        for k in range(n_tile):
+            cols = slice(k * f_blk, (k + 1) * f_blk)
+            back = jnp.dot(act[...], w1[v, :, k].reshape(n_blk * f_blk, f_blk), preferred_element_type=F32)
+            go[v, m, :, cols] = (gb[v, m, :, cols].astype(F32) + back).astype(BF16)
         done = first & (v == 0)
 
         @pl.when(done)
@@ -297,6 +314,10 @@
         b_k, b_m = lax.div(b_pos, n_stage), lax.rem(b_pos, n_stage)
         b_on = (behind >= 0) & (b_k < 2) & (b_m < CHUNKS)
 
+        @pl.when(t == CHUNKS)
+        def _():
+            weights[1].step_far()
+
         @pl.when(t == n_stage)
         def _():
             weights[1].step_relay()
@@ -308,6 +329,10 @@
         @pl.when(f_on)
         def _():
             forward(f_v, f_m)
+
+        @pl.when(f_on & (f_m == CHUNKS - 1))
+        def _():
+            transpose(f_v)
 
         @pl.when(b_on)
         def _():
@@ -334,9 +359,6 @@
         unit.step_last()
     for keep in keeps:
         keep.wait()
-    for v in range(2):
-        for part, buf in zip(weights[v].parts, (w1, w2)):
-            part.step_sent(buf.at[v, pl.ds(0, n_inner - 1)])
     for unit, (v, out) in zip(acts, ((0, h_all), (1, h_all), (1, g_all), (0, g_all))):
         for colour, part in enumerate(unit.parts):
             part.step_sent(out.at[v, pl.ds(0, n_inner - 1), pl.ds(colour * rows, rows)])
@@ -421,15 +443,15 @@
             in_specs=[any_spec] * 4,
             out_specs=(any_spec,) * 4,
             scratch_shapes=[
-                pltpu.VMEM((2, n_inner, d_model, f_blk), BF16),
-                pltpu.VMEM((2, n_inner, f_blk, d_model), BF16),
+                pltpu.VMEM((2, n_inner, d_model // f_blk, f_blk, f_blk), BF16),
+                pltpu.VMEM((2, n_inner, d_model // f_blk, f_blk, f_blk), BF16),
                 pltpu.VMEM((2, CHUNKS, rows, f_full), F32),
                 pltpu.VMEM((rows, f_full), BF16),
                 pltpu.VMEM((2, CHUNKS, rows, d_model), BF16),
                 pltpu.VMEM((2, CHUNKS, rows, d_model), BF16),
                 pltpu.VMEM((2, CHUNKS, rows, d_model), BF16),
                 pltpu.VMEM((2, CHUNKS, rows, d_model), BF16),
-                dma((2, 2)), dma((2, 2, CHUNKS)), dma((6, 2, 20)), dma((6, 2)),
+                dma((2, 2, d_model // f_blk)), dma((2, 2, CHUNKS)), dma((6, 2, 20)), dma((6, 2)),
                 dma((n_stage,)), dma((1,)), dma((n_stage,)), dma((1,)),
                 dma((2, CHUNKS)), dma((2, CHUNKS)), dma((2, CHUNKS)), dma((2, CHUNKS)),
                 dma((1,)), dma((n_stage,)), dma((1,)), dma((n_stage,)),

time: 479 us -> 451 us (0.942)
  Pallas kernels: 473 us -> 444 us
    pallas_call x1, Pallas kernels: 444 us -> 415 us  [device_step(): pl.pallas_call(functools.partial(main_kernel, n_stage), name='stack', out...]
where the time goes in v2:
time: 451 us; the launch traced here: 449 us
  Pallas kernels  444 us (98%)
    pallas_call x1, Pallas kernels, device_step(): pl.pallas_call(functools.partial(main_kernel, n_stage), name='stack', out...  415 us
    pallas_call x1, Pallas kernels, device_step(): pl.pallas_call(grad_kernel, name='grads', grid=(2, tokens // blk), out_sh...  28.9 us

profile of v2, /device:TPU:8, one launch (start us, length us, event | category | flops | bytes accessed | tf_op | source)
XLA Modules:
  0.0 448.6 jit_solution(2081570197510366588)
XLA Ops:
  0.6 415.3 %stack.1 = (bf16[1,32,1024]{2,1,0:T(8,128)(2,1)}, bf16[1,32,1024]{2,1,0:T(8,128)(2,1)}, bf16[2,16,256,1024]{3,2,1,0:T(8,128)(2,1)}, bf16[2,16,256,1024]{3,2,1,0:T(8,128)(2,1)}) custom-call(bf16[1,32,1024]{2,1,0:T(8,128)(2,1)} %x_ref.1, bf16[1,32,1024]{2,1,0:T(8,128)(2,1)} %g_ref.1, bf16[2,1,1024,256]{3,2,1,0:T(8,128)(2,1)} %wu_ref.3, ...), custom_call_target="tpu_custom_call" | custom-call | tf_op jit(solution)/shard_map/stack/pallas_call | solution.py:437
  415.9 0.0 copy-start
  415.9 1.2 copy-done
  417.1 0.0 copy-start.1
  417.1 1.2 copy-done.1
  418.4 0.0 copy-start.3
  418.4 0.0 copy-start.2
  418.4 28.9 %grads.1 = (f32[2,1,1024,256]{3,2,1,0:T(8,128)}, f32[2,1,256,1024]{3,2,1,0:T(8,128)}) custom-call(bf16[2,4096,1024]{2,1,0:T(8,128)(2,1)} %bitcast.2, bf16[2,4096,1024]{2,1,0:T(8,128)(2,1)} %bitcast.3, bf16[2,1,1024,256]{3,2,1,0:T(8,128)(2,1)S(1)} %copy-done, bf16[2,1,256,1024]{3,2,1,0:T(8,128)(2,1)S(1)} %copy-done.1), custom_call_target="tpu_custom_call" | custom-call | tf_op jit(solution)/shard_map/grads/pallas_call | solution.py:467
  447.3 0.0 copy-done.3
  447.3 0.6 copy.10
  447.9 0.0 copy-done.2
  447.9 0.6 copy.11
Async XLA Ops:
  415.9 1.2 copy-start
  417.1 1.2 copy-start.1
  418.4 28.9 %copy-start.3 = (bf16[1,32,1024]{2,1,0:T(8,128)(2,1)S(1)}, bf16[1,32,1024]{2,1,0:T(8,128)(2,1)}, u32[]{:S(2)}) copy-start(bf16[1,32,1024]{2,1,0:T(8,128)(2,1)} %get-tuple-element.20) | copy-start | bytes 196612
  418.4 29.6 %copy-start.2 = (bf16[1,32,1024]{2,1,0:T(8,128)(2,1)S(1)}, bf16[1,32,1024]{2,1,0:T(8,128)(2,1)}, u32[]{:S(2)}) copy-start(bf16[1,32,1024]{2,1,0:T(8,128)(2,1)} %get-tuple-element.21) | copy-start | bytes 196612

commit v3 on v0

v3 whole, which is shorter than its diff:
```python
import functools

import jax
import jax.numpy as jnp
from jax import lax
from jax.experimental import pallas as pl
from jax.experimental.pallas import tpu as pltpu
from jax.sharding import PartitionSpec as P

MESH = pl.DeviceIdType.MESH
NT = (((1,), (1,)), ((), ()))
TN = (((0,), (0,)), ((), ()))
SIDE = 4
F32 = jnp.float32
BF16 = jnp.bfloat16


def gelu_parts(pre_act):
    normal_cdf = 0.5 * (1.0 + lax.erf(pre_act * 0.7071067811865476))
    normal_pdf = jnp.exp(-0.5 * pre_act * pre_act) * 0.3989422804014327
    return normal_cdf, normal_pdf


class Place:
    def __init__(self, n_stage):
        inner, stage = lax.axis_index('inner'), lax.axis_index('stage')
        self.n_x = n_stage // 2
        self.z, self.y = lax.div(inner, SIDE), lax.rem(inner, SIDE)
        self.x, self.core = lax.div(stage, 2), lax.rem(stage, 2)
        self.column = lax.div(self.y, 2)
        self.role = lax.rem(self.column + self.x, 2)
        self.level = 2 * self.x + self.role
        self.key = jnp.where(self.y < 2, self.y, 3 - self.y)
        self.pair_y = self.y + 1 - 2 * lax.rem(self.y, 2)
        self.mate_y = 3 - self.y

    def at(self, x=None, y=None, z=None, core=None):
        x, y = self.x if x is None else x, self.y if y is None else y
        z, core = self.z if z is None else z, self.core if core is None else core
        return {'inner': z * SIDE + y, 'stage': x * 2 + core}

    def z_off(self, off):
        return lax.rem(self.z + off + SIDE, SIDE)


def remote(src, dst, send_sem, recv_sem, where):
    return pltpu.make_async_remote_copy(src_ref=src, dst_ref=dst, send_sem=send_sem, recv_sem=recv_sem,
                                        device_id=where, device_id_type=MESH)


class Gather:
    def __init__(self, place, core, slot, own, arrive, share, ici_sem, d2d_sem):
        self.place, self.core, self.slot, self.own = place, core, slot, own
        self.arrive, self.share, self.ici_sem, self.d2d_sem = arrive, share, ici_sem, d2d_sem

    def piece(self, d_z, d_k):
        place = self.place
        return place.z_off((0, -1, 1, 2)[d_z]), place.key if d_k == 0 else 1 - place.key

    def ref(self, d_z, d_k, half=None):
        if d_z == 0 and d_k == 0:
            return self.own(half)
        return self.slot(*self.piece(d_z, d_k), half)

    def send(self, d_z, d_k, half, where, as_z, as_k):
        sem = self.arrive((as_z * 2 + as_k) * 2 + (half or 0))
        remote(self.ref(d_z, d_k, half), self.slot(*self.piece(d_z, d_k), half), self.ici_sem, sem, where).start()

    def to_pair(self, d_z, half=None):
        self.send(d_z, 0, half, self.place.at(y=self.place.pair_y), d_z, 1)

    def to_z(self, d_k, up):
        self.send(0, d_k, None, self.place.at(z=self.place.z_off(1 if up else -1)), 1 if up else 2, d_k)

    def across_z(self, d_z, d_k):
        half, off = (0, 1) if d_z == 1 else (1, -1)
        self.send(d_z, d_k, half, self.place.at(z=self.place.z_off(off)), 3, d_k)

    def wait(self, d_z, d_k, half=None):
        ref = self.slot(*self.piece(d_z, d_k), half)
        sem = self.arrive((d_z * 2 + d_k) * 2 + (half or 0))
        remote(ref, ref, self.ici_sem, sem, self.place.at()).wait_recv()

    def pass_on(self, d_z, d_k, half=None):
        sem = self.share((d_z * 2 + d_k) * 2 + (half or 0))
        remote(self.ref(d_z, d_k, half), self.slot(*self.piece(d_z, d_k), half), self.d2d_sem, sem,
               self.place.at(core=1 - self.place.core)).start()

    def start(self):
        if self.core == 0:
            self.to_pair(0)
            self.to_z(0, True)
            self.to_z(0, False)
        else:
            self.to_z(0, True)
            self.to_z(0, False)
            self.to_pair(0)

    def near(self):
        if self.core == 0:
            self.wait(0, 1)
            self.to_z(1, True)
            self.to_z(1, False)
            self.pass_on(0, 1)
        else:
            for d_z in (1, 2):
                self.wait(d_z, 0)
                self.across_z(d_z, 0)
                self.to_pair(d_z)
                self.pass_on(d_z, 0)

    def relay(self):
        if self.core == 0:
            for d_k in (0, 1):
                for d_z in (1, 2):
                    self.wait(d_z, d_k)
                    self.across_z(d_z, d_k)
                    self.pass_on(d_z, d_k)
        else:
            for half in (0, 1):
                self.wait(3, 0, half)
            self.to_pair(3)
            self.pass_on(3, 0)

    def last(self):
        if self.core == 0:
            for d_k in (0, 1):
                for half in (0, 1):
                    self.wait(3, d_k, half)
                    self.pass_on(3, d_k, half)
        else:
            for d_z in range(4):
                self.wait(d_z, 1)
                self.pass_on(d_z, 1)

    def shared(self):
        for d_z in range(4):
            for d_k in range(2):
                if d_z == 0 and d_k == 0:
                    continue
                for half in ((0, 1) if d_z == 3 and self.core == 0 else (None,)):
                    ref = self.slot(*self.piece(d_z, d_k), half)
                    sem = self.share((d_z * 2 + d_k) * 2 + (half or 0))
                    remote(ref, ref, self.ici_sem, sem, self.place.at()).wait_recv()

    def sent(self, seven):
        remote(seven, seven, self.ici_sem, self.arrive(0), self.place.at()).wait_send()
        remote(seven, seven, self.d2d_sem, self.arrive(0), self.place.at()).wait_send()


class ByCore:
    def __init__(self, tag, place, gathers):
        self.tag, self.place, self.gathers = tag, place, gathers

    def step(self, name):
        for core in range(2):
            @pl.when(self.place.core == core)
            def _():
                with jax.named_scope(f'{self.tag}_{name}'):
                    getattr(self.gathers[core], name)()

    def shared(self):
        for core in range(2):
            @pl.when(self.place.core == core)
            def _():
                with jax.named_scope(f'{self.tag}_shared'):
                    self.gathers[1 - core].shared()

    def sent(self, sevens):
        for core in range(2):
            @pl.when(self.place.core == core)
            def _():
                self.gathers[core].sent(sevens[core])


def main_kernel(n_stage, x_ref, g_ref, wu_ref, wd_ref, y_ref, dx_ref, h_all, g_all, b1_ref, b2_ref,
                w1, w2, zb, act, hb, gb, ho, go,
                load_sem, mate_sem, mate_send, twin_sem, twin_send, arrive, share, ici, d2d,
                keep_sem, own_sem, own_send, blk_sem,
                xr, xs, gr, gs, fr, fs, br, bs, yr, ys, dr, ds):
    place = Place(n_stage)
    core, role, level = place.core, place.role, place.level
    first, last = level == 0, level == n_stage - 1
    n_blk, n_tile, f_blk = w1.shape[1:4]
    d_model = n_tile * f_blk
    tok = x_ref.shape[1]
    n_chunk = hb.shape[1]
    own_slot = place.z * SIDE + place.key * 2 + place.column
    mate_slot = place.z * SIDE + place.key * 2 + 1 - place.column
    matched = core == role
    twin = place.at(core=1 - core)

    @pl.when(matched)
    def _():
        for v in range(2):
            for k in range(n_tile):
                part = pl.ds(k * f_blk, f_blk)
                pltpu.make_async_copy(wu_ref.at[v, 0, part], w1.at[v, own_slot, k], load_sem.at[v, 0]).start()
                pltpu.make_async_copy(wd_ref.at[v, 0, :, part], w2.at[v, own_slot, k], load_sem.at[v, 1]).start()

    barrier = pltpu.get_barrier_semaphore()
    peers = [twin, place.at(y=place.pair_y), place.at(z=place.z_off(1)), place.at(z=place.z_off(-1)),
             place.at(y=place.mate_y, core=1 - core)]
    for off in range(place.n_x):
        x = lax.rem(place.x + off, place.n_x)
        peers.append(place.at(x=x, y=place.mate_y))
        if off:
            peers.append(place.at(x=x))
    for peer in peers:
        pl.semaphore_signal(barrier, inc=1, device_id=peer, device_id_type=MESH)
    with jax.named_scope('barrier'):
        pl.semaphore_wait(barrier, len(peers))

    @pl.when(jnp.logical_not(matched))
    def _():
        for v in range(2):
            for k in range(n_tile):
                part = pl.ds(k * f_blk, f_blk)
                remote(wu_ref.at[v, 0, part], w1.at[v, own_slot, k], mate_send.at[v, 0], mate_sem.at[v],
                       place.at(y=place.mate_y, core=0)).start()
                remote(wd_ref.at[v, 0, :, part], w2.at[v, own_slot, k], mate_send.at[v, 1], mate_sem.at[v],
                       place.at(y=place.mate_y, core=1)).start()

    def own_blocks(v):
        @pl.when(matched)
        def _():
            for colour, buf in enumerate((w1, w2)):
                ref = buf.at[v, own_slot]
                remote(ref, ref, twin_send.at[0, 0, 0], load_sem.at[v, colour], twin).wait_recv()
                remote(ref, ref, twin_send.at[v, colour, 0], twin_sem.at[v, colour, 0], twin).start()

        @pl.when(jnp.logical_not(matched))
        def _():
            for colour, buf in enumerate((w1, w2)):
                ref = buf.at[v, own_slot]
                remote(ref, ref, twin_send.at[0, 0, 0], twin_sem.at[v, colour, 0], twin).wait_recv()

        for colour, buf in enumerate((w1, w2)):
            @pl.when(core == colour)
            def _():
                ref = buf.at[v, mate_slot]
                remote(ref, ref, twin_send.at[0, 0, 0], mate_sem.at[v], twin).wait_recv()
                remote(ref, ref, twin_send.at[v, colour, 1], twin_sem.at[v, colour, 1], twin).start()

    def weights_of(v):
        gathers = []
        for colour, buf in enumerate((w1, w2)):
            def slot(z, key, half, buf=buf):
                base = z * SIDE + key * 2
                return buf.at[v, pl.ds(base, 2)] if half is None else buf.at[v, pl.ds(base + half, 1)]

            gathers.append(Gather(place, colour, slot, functools.partial(slot, place.z, place.key),
                                  lambda k: arrive.at[v, k], lambda k: share.at[v, k], ici.at[v], d2d.at[v]))
        return ByCore(f'w{v}', place, gathers)

    def lanes_of(tag, unit, buf, out, v, base, count):
        gathers = []
        for colour in range(2):
            def part(half):
                return pl.ds(base, count) if half is None else pl.ds(base + half * (count // 2), count // 2)

            def slot(z, key, half, colour=colour):
                return out.at[v, colour, z * 2 + key, part(half)]

            gathers.append(Gather(place, colour, slot, lambda half: buf.at[v, part(half)],
                                  lambda k: arrive.at[unit, k], lambda k: share.at[unit, k], ici.at[unit], d2d.at[unit]))
        return ByCore(tag, place, gathers)

    half_lane = n_chunk // 2
    weights = [weights_of(0), weights_of(1)]

    def weights_here(v):
        weights[v].shared()
        for colour, buf in enumerate((w1, w2)):
            @pl.when(core != colour)
            def _():
                ref = buf.at[v, mate_slot]
                remote(ref, ref, twin_send.at[0, 0, 0], twin_sem.at[v, colour, 1], twin).wait_recv()
    h0 = lanes_of('h0', 2, hb, h_all, 0, 0, n_chunk)
    h1 = lanes_of('h1', 3, hb, h_all, 1, 0, n_chunk)
    g1 = lanes_of('g1', 4, gb, g_all, 1, 0, n_chunk)
    g0a = lanes_of('g0a', 5, gb, g_all, 0, 0, half_lane)
    g0b = lanes_of('g0b', 6, gb, g_all, 0, half_lane, half_lane)

    def keep(k, v, base, count):
        buf, out = ((hb, h_all), (gb, g_all))[k]
        idx = 0 if base == 0 else 1
        part = pl.ds(base, count)
        for colour in range(2):
            @pl.when(core == colour)
            def _():
                dst = out.at[v, colour, place.z * 2 + place.key, part]
                pltpu.make_async_copy(buf.at[v, part], dst, keep_sem.at[k, v, idx]).start()
                remote(buf.at[v, part], dst, own_send.at[k, v, idx], own_sem.at[k, v, idx], twin).start()

    def kept(k, v, base, count):
        buf, out = ((hb, h_all), (gb, g_all))[k]
        idx = 0 if base == 0 else 1
        part = pl.ds(base, count)
        for colour in range(2):
            @pl.when(core == colour)
            def _():
                mine = out.at[v, colour, place.z * 2 + place.key, part]
                other = out.at[v, 1 - colour, place.z * 2 + place.key, part]
                pltpu.make_async_copy(buf.at[v, part], mine, keep_sem.at[k, v, idx]).wait()
                remote(buf.at[v, part], other, own_send.at[k, v, idx], own_sem.at[k, v, idx], twin).wait()

    micro = 2 * place.x + place.column
    x_dst, g_dst = hb.at[0, micro], gb.at[1, micro]

    @pl.when(first)
    def _():
        pltpu.make_async_copy(x_ref.at[0], x_dst, xr.at[micro]).start()

    @pl.when(jnp.logical_not(first))
    def _():
        remote(x_ref.at[0], x_dst, xs.at[0], xr.at[micro], place.at(x=0, y=place.key)).start()

    @pl.when(last)
    def _():
        pltpu.make_async_copy(g_ref.at[0], g_dst, gr.at[micro]).start()

    @pl.when(jnp.logical_not(last))
    def _():
        remote(g_ref.at[0], g_dst, gs.at[0], gr.at[micro], place.at(x=place.n_x - 1, y=place.key)).start()

    own_blocks(0)
    weights[0].step('start')
    own_blocks(1)
    weights[0].step('near')
    weights[1].step('start')
    weights[0].step('relay')
    weights[1].step('near')
    weights[0].step('last')
    weights_here(0)

    def wait_in(buf, v, m, ready, micro_ready, from_tokens):
        ref = buf.at[v, m]

        @pl.when(from_tokens)
        def _():
            remote(ref, ref, xs.at[0], micro_ready.at[m], twin).wait_recv()

        @pl.when(jnp.logical_not(from_tokens))
        def _():
            remote(ref, ref, xs.at[0], ready.at[v, m], twin).wait_recv()

    def give_out(src, m, out_ref, sends, recv):
        home_x = lax.div(m, 2)
        home_y = jnp.where(lax.rem(m, 2) == 0, place.key, 3 - place.key)
        here = (home_x == place.x) & (home_y == place.y)

        @pl.when(here)
        def _():
            pltpu.make_async_copy(src, out_ref.at[0], recv.at[0]).start()

        @pl.when(jnp.logical_not(here))
        def _():
            remote(src, out_ref.at[0], sends.at[m], recv.at[0], place.at(x=home_x, y=home_y)).start()

    up_x = lax.rem(place.x + role, place.n_x)
    up_y = jnp.where(role == 0, place.mate_y, place.y)
    down_x = lax.rem(place.x + place.n_x - 1 + role, place.n_x)
    down_y = jnp.where(role == 1, place.mate_y, place.y)

    def forward(v, m):
        with jax.named_scope('f_wait'):
            wait_in(hb, v, m, fr, xr, first & (v == 0))
        h_in = hb[v, m]
        for blk in range(n_blk):
            cols = slice(blk * f_blk, (blk + 1) * f_blk)
            pre_act = jnp.dot(h_in, w1[v, blk].reshape(d_model, f_blk), preferred_element_type=F32)
            zb[v, m, :, cols] = pre_act
            normal_cdf = 0.5 * (1.0 + lax.erf(pre_act * 0.7071067811865476))
            act[:, cols] = (pre_act * normal_cdf).astype(BF16)
        for k in range(n_tile):
            cols = slice(k * f_blk, (k + 1) * f_blk)
            branch = jnp.dot(act[...], w2[v, :, k].reshape(n_blk * f_blk, f_blk), preferred_element_type=F32)
            ho[v, m, :, cols] = (hb[v, m, :, cols].astype(F32) + branch).astype(BF16)
        done = last & (v == 1)

        @pl.when(done)
        def _():
            give_out(ho.at[v, m], m, y_ref, ys, yr)

        @pl.when(jnp.logical_not(done))
        def _():
            v_to = v + last.astype(jnp.int32)
            remote(ho.at[v, m], hb.at[v_to, m], fs.at[v, m], fr.at[v_to, m], place.at(x=up_x, y=up_y)).start()

    def transpose(v):
        for u in range(2):
            @pl.when(v == u)
            def _():
                for colour, (buf, out) in enumerate(((w1, b1_ref), (w2, b2_ref))):
                    mine = jnp.where(matched, own_slot, mate_slot)
                    copy = pltpu.make_async_copy(buf.at[u, mine], out.at[u], blk_sem.at[u, colour])
                    copy.start()
                weights[u].sent((w1.at[u, pl.ds(0, 14)], w2.at[u, pl.ds(0, 14)]))
                for colour, (buf, out) in enumerate(((w1, b1_ref), (w2, b2_ref))):
                    @pl.when(matched)
                    def _():
                        ref = buf.at[u, own_slot]
                        remote(ref, ref, twin_send.at[u, colour, 0], twin_sem.at[u, colour, 0], twin).wait_send()

                    @pl.when(core == colour)
                    def _():
                        ref = buf.at[u, mate_slot]
                        remote(ref, ref, twin_send.at[u, colour, 1], twin_sem.at[u, colour, 1], twin).wait_send()

                    pltpu.make_async_copy(buf.at[u, own_slot], out.at[u], blk_sem.at[u, colour]).wait()

        def tiles(blk, carry):
            for buf in (w2, w1):
                for k in range(n_tile):
                    buf[v, blk, k] = buf[v, blk, k].T
            return carry

        with jax.named_scope('transpose'):
            lax.fori_loop(0, n_blk, tiles, 0)

    def backward(v, m):
        with jax.named_scope('b_wait'):
            wait_in(gb, v, m, br, gr, last & (v == 1))
        g_out = gb[v, m]
        for blk in range(n_blk):
            cols = slice(blk * f_blk, (blk + 1) * f_blk)
            d_act = jnp.dot(g_out, w2[v, blk].reshape(d_model, f_blk), preferred_element_type=F32)
            pre_act = zb[v, m, :, cols]
            normal_cdf, normal_pdf = gelu_parts(pre_act)
            act[:, cols] = (d_act * (normal_cdf + pre_act * normal_pdf)).astype(BF16)
        for k in range(n_tile):
            cols = slice(k * f_blk, (k + 1) * f_blk)
            back = jnp.dot(act[...], w1[v, :, k].reshape(n_blk * f_blk, f_blk), preferred_element_type=F32)
            go[v, m, :, cols] = (gb[v, m, :, cols].astype(F32) + back).astype(BF16)
        done = first & (v == 0)

        @pl.when(done)
        def _():
            give_out(go.at[v, m], m, dx_ref, ds, dr)

        @pl.when(jnp.logical_not(done))
        def _():
            v_to = v - first.astype(jnp.int32)
            remote(go.at[v, m], gb.at[v_to, m], bs.at[v, m], br.at[v_to, m], place.at(x=down_x, y=down_y)).start()

    f0 = level
    b0 = 2 * n_stage + n_chunk - 1 + (n_stage - 1 - level)
    f1, b1 = f0 + n_stage, b0 + n_stage

    def tick(t, carry):
        f_pos = jnp.maximum(t - f0, 0)
        f_v, f_m = lax.div(f_pos, n_stage), lax.rem(f_pos, n_stage)
        f_on = (t >= f0) & (f_v < 2) & (f_m < n_chunk)
        b_pos = jnp.maximum(t - b0, 0)
        b_k, b_m = lax.div(b_pos, n_stage), lax.rem(b_pos, n_stage)
        b_on = (t >= b0) & (b_k < 2) & (b_m < n_chunk)

        def at(when, *steps):
            @pl.when(t == when)
            def _():
                for step in steps:
                    step()

        at(f1,
           lambda: weights[1].step('relay'),
           lambda: transpose(0),
           lambda: weights[1].step('last'),
           lambda: weights_here(1),
           lambda: h0.step('start'),
           lambda: keep(0, 0, 0, n_chunk))
        at(b1,
           lambda: g1.step('start'),
           lambda: keep(1, 1, 0, n_chunk),
           lambda: g1.step('near'))

        @pl.when(f_on)
        def _():
            forward(f_v, f_m)

        at(f1 + n_chunk - 1, lambda: transpose(1))

        @pl.when(b_on)
        def _():
            backward(1 - b_k, b_m)

        at(f1 + n_chunk // 2, lambda: h0.step('near'))
        at(f1 + n_chunk,
           lambda: h0.step('relay'),
           lambda: h1.step('start'),
           lambda: keep(0, 1, 0, n_chunk))
        at(f1 + n_chunk + n_chunk // 2, lambda: h0.step('last'), lambda: h1.step('near'))
        at(f1 + 2 * n_chunk - 1, lambda: h1.step('relay'))
        at(b1 + n_chunk // 2 - 1, lambda: g1.step('relay'), lambda: h1.step('last'))
        at(b1 + n_chunk // 2, lambda: g0a.step('start'), lambda: keep(1, 0, 0, half_lane))
        at(b1 + n_chunk - 1,
           lambda: g0a.step('near'),
           lambda: g0b.step('start'),
           lambda: keep(1, 0, half_lane, half_lane),
           lambda: g1.step('last'),
           lambda: g0a.step('relay'),
           lambda: g0b.step('near'),
           lambda: g0a.step('last'),
           lambda: g0b.step('relay'),
           lambda: g0b.step('last'))
        return carry

    lax.fori_loop(0, 4 * n_stage + 2 * n_chunk, tick, 0)

    for unit in (h0, h1, g1, g0a, g0b):
        unit.shared()
    for k, v, base, count in ((0, 0, 0, n_chunk), (0, 1, 0, n_chunk), (1, 1, 0, n_chunk),
                              (1, 0, 0, half_lane), (1, 0, half_lane, half_lane)):
        kept(k, v, base, count)
    seven = pl.ds(0, 7)
    for unit, out, v, part in ((h0, h_all, 0, pl.ds(0, n_chunk)), (h1, h_all, 1, pl.ds(0, n_chunk)), (g1, g_all, 1, pl.ds(0, n_chunk)),
                               (g0a, g_all, 0, pl.ds(0, half_lane)), (g0b, g_all, 0, pl.ds(half_lane, half_lane))):
        unit.sent((out.at[v, 0, seven, part], out.at[v, 1, seven, part]))

    def wait_sent(ref, sem):
        remote(ref, ref, sem, xr.at[0], twin).wait_send()

    @pl.when(jnp.logical_not(matched))
    def _():
        for v in range(2):
            for colour, buf in enumerate((w1, w2)):
                wait_sent(buf.at[v, 0], mate_send.at[v, colour])

    @pl.when(jnp.logical_not(first))
    def _():
        wait_sent(x_ref.at[0], xs.at[0])

    @pl.when(jnp.logical_not(last))
    def _():
        wait_sent(g_ref.at[0], gs.at[0])

    for m in range(n_chunk):
        home_x = m // 2
        home_y = jnp.where(m % 2 == 0, place.key, 3 - place.key)
        here = (home_x == place.x) & (home_y == place.y)
        for v in range(2):
            ends, starts = last & (v == 1), first & (v == 0)

            @pl.when(jnp.logical_not(ends))
            def _():
                wait_sent(ho.at[v, m], fs.at[v, m])

            @pl.when(jnp.logical_not(starts))
            def _():
                wait_sent(go.at[v, m], bs.at[v, m])

        @pl.when(last & jnp.logical_not(here))
        def _():
            wait_sent(ho.at[1, m], ys.at[m])

        @pl.when(first & jnp.logical_not(here))
        def _():
            wait_sent(go.at[0, m], ds.at[m])

    remote(y_ref.at[0], y_ref.at[0], xs.at[0], yr.at[0], twin).wait_recv()
    remote(dx_ref.at[0], dx_ref.at[0], xs.at[0], dr.at[0], twin).wait_recv()


def grad_kernel(n_stage, h_ref, g_ref, b1_ref, b2_ref, du_ref, dd_ref, acc_u, acc_d, out_u, send_sem, recv_sem):
    place = Place(n_stage)
    mate = place.at(y=place.mate_y, core=1 - place.core)
    matched = place.core == place.role
    group, step = 1 - pl.program_id(0), pl.program_id(1)
    end = pl.num_programs(1) - 1
    n_tile, f_blk = b1_ref.shape[1:3]
    d_model = n_tile * f_blk
    rows = h_ref.shape[1] * h_ref.shape[2] * h_ref.shape[3]

    @pl.when((group == 1) & (step == 0))
    def _():
        barrier = pltpu.get_barrier_semaphore()
        pl.semaphore_signal(barrier, inc=1, device_id=mate, device_id_type=MESH)
        pl.semaphore_wait(barrier, 1)

    @pl.when(step == 0)
    def _():
        acc_u[...] = jnp.zeros_like(acc_u)
        acc_d[group] = jnp.zeros_like(acc_d[group])

    h_in = h_ref[...].reshape(rows, d_model)
    g_out = g_ref[...].reshape(rows, d_model)
    pre_act = jnp.dot(h_in, b1_ref[0].reshape(d_model, f_blk), preferred_element_type=F32)
    d_act = None
    for k in range(n_tile):
        term = lax.dot_general(g_out[:, k * f_blk:(k + 1) * f_blk], b2_ref[0, k], NT, preferred_element_type=F32)
        d_act = term if d_act is None else d_act + term
    normal_cdf, normal_pdf = gelu_parts(pre_act)
    act_val = (pre_act * normal_cdf).astype(BF16)
    d_pre = (d_act * (normal_cdf + pre_act * normal_pdf)).astype(BF16)
    acc_u[...] += lax.dot_general(d_pre, h_in, TN, preferred_element_type=F32)
    acc_d[group] += lax.dot_general(act_val, g_out, TN, preferred_element_type=F32)

    def give(v, start):
        for k, (src, dst) in enumerate(((acc_d.at[v], dd_ref.at[v, 0]), (out_u.at[v], du_ref.at[v, 0]))):
            @pl.when(matched)
            def _():
                copy = pltpu.make_async_copy(src, dst, recv_sem.at[v, k])
                copy.start() if start else copy.wait()

            @pl.when(jnp.logical_not(matched))
            def _():
                copy = remote(src, dst, send_sem.at[v, k], recv_sem.at[v, k], mate)
                copy.start() if start else copy.wait()

    for v in range(2):
        @pl.when((group == v) & (step == end))
        def _():
            out_u[v] = acc_u[...].T
            give(v, True)

    @pl.when((group == 0) & (step == end))
    def _():
        for v in range(2):
            give(v, False)


def solution(mesh):
    n_stage = mesh.shape['stage']
    n_inner = mesh.shape['inner']
    tok_spec = P(('data', 'stage', 'inner'))
    up_spec = P(None, ('data', 'stage'), None, 'inner')
    down_spec = P(None, ('data', 'stage'), 'inner', None)

    def device_step(x_loc, g_loc, w_up, w_down):
        tok, d_model = x_loc.shape[1:]
        f_blk = w_up.shape[3]
        n_tile = d_model // f_blk
        n_chunk = n_stage
        f_full = n_inner * f_blk
        any_spec = pl.BlockSpec(memory_space=pl.ANY)
        dma = pltpu.SemaphoreType.DMA
        lanes = jax.ShapeDtypeStruct((2, 2, n_inner // 2, n_chunk, tok, d_model), BF16)
        blocks = jax.ShapeDtypeStruct((2, n_tile, f_blk, f_blk), BF16)
        y_loc, dx_loc, h_all, g_all, b1, b2 = pl.pallas_call(
            functools.partial(main_kernel, n_stage),
            name='stack',
            out_shape=(jax.ShapeDtypeStruct(x_loc.shape, BF16), jax.ShapeDtypeStruct(x_loc.shape, BF16),
                       lanes, lanes, blocks, blocks),
            in_specs=[any_spec] * 4,
            out_specs=(any_spec,) * 6,
            scratch_shapes=[
                pltpu.VMEM((2, n_inner, n_tile, f_blk, f_blk), BF16),
                pltpu.VMEM((2, n_inner, n_tile, f_blk, f_blk), BF16),
                pltpu.VMEM((2, n_chunk, tok, f_full), F32),
                pltpu.VMEM((tok, f_full), BF16),
                pltpu.VMEM((2, n_chunk, tok, d_model), BF16),
                pltpu.VMEM((2, n_chunk, tok, d_model), BF16),
                pltpu.VMEM((2, n_chunk, tok, d_model), BF16),
                pltpu.VMEM((2, n_chunk, tok, d_model), BF16),
                dma((2, 2)), dma((2,)), dma((2, 2)), dma((2, 2, 2)), dma((2, 2, 2)),
                dma((7, 16)), dma((7, 16)), dma((7,)), dma((7,)),
                dma((2, 2, 2)), dma((2, 2, 2)), dma((2, 2, 2)), dma((2, 2)),
                dma((n_chunk,)), dma((1,)), dma((n_chunk,)), dma((1,)),
                dma((2, n_chunk)), dma((2, n_chunk)), dma((2, n_chunk)), dma((2, n_chunk)),
                dma((1,)), dma((n_chunk,)), dma((1,)), dma((n_chunk,)),
            ],
            compiler_params=pltpu.CompilerParams(
                collective_id=0, has_side_effects=True, vmem_limit_bytes=60 << 20),
        )(x_loc, g_loc, w_up, w_down)

        h_all = h_all.reshape(2, n_inner, n_chunk, tok, d_model)
        g_all = g_all.reshape(2, n_inner, n_chunk, tok, d_model)
        lane_spec = pl.BlockSpec((1, 2, n_chunk, tok, d_model), lambda v, t: (1 - v, t, 0, 0, 0))
        block_spec = pl.BlockSpec((1, n_tile, f_blk, f_blk), lambda v, t: (1 - v, 0, 0, 0))
        dw_up, dw_down = pl.pallas_call(
            functools.partial(grad_kernel, n_stage),
            name='grads',
            grid=(2, n_inner // 2),
            out_shape=(jax.ShapeDtypeStruct(w_up.shape, F32), jax.ShapeDtypeStruct(w_down.shape, F32)),
            in_specs=[lane_spec, lane_spec, block_spec, block_spec],
            out_specs=(any_spec, any_spec),
            scratch_shapes=[pltpu.VMEM((f_blk, d_model), F32), pltpu.VMEM((2, f_blk, d_model), F32),
                            pltpu.VMEM((2, d_model, f_blk), F32), dma((2, 2)), dma((2, 2))],
            compiler_params=pltpu.CompilerParams(
                dimension_semantics=('arbitrary', 'arbitrary'), collective_id=1, has_side_effects=True,
                vmem_limit_bytes=40 << 20),
        )(h_all, g_all, b1, b2)
        return y_loc, dx_loc, dw_up, dw_down

    return jax.shard_map(device_step, mesh=mesh, in_specs=(tok_spec, tok_spec, up_spec, down_spec),
                         out_specs=(tok_spec, tok_spec, up_spec, down_spec), check_vma=False)
```

time: 2250 us -> 461 us (0.20)
  the two profiles are of different devices: /device:TPU:8 before, /device:TPU:1 now
where the time goes in v3:
time: 461 us
  Pallas kernels  454 us (98%)
  local copies, waits for them, and re-layouts  6.35 us (1%)
    pallas_call x1, Pallas kernels, device_step(): pl.pallas_call(functools.partial(main_kernel, n_stage), name='stack', out...  390 us
    pallas_call x1, Pallas kernels, device_step(): pl.pallas_call(functools.partial(grad_kernel, n_stage), name='grads', gri...  63.7 us

profile of v3, /device:TPU:1, one launch (start us, length us, event | category | flops | bytes accessed | tf_op | source)
XLA Modules:
  0.0 460.8 jit_solution(5666760615613334815)
XLA Ops:
  0.6 390.1 %stack.1 = (bf16[1,32,1024]{2,1,0:T(8,128)(2,1)}, bf16[1,32,1024]{2,1,0:T(8,128)(2,1)}, bf16[2,2,8,8,32,1024]{5,4,3,2,1,0:T(8,128)(2,1)}, bf16[2,2,8,8,32,1024]{...) custom-call(bf16[1,32,1024]{2,1,0:T(8,128)(2,1)} %x_ref.1, ...), custom_call_target="tpu_custom_call" | custom-call | tf_op jit(solution)/shard_map/stack/pallas_call | solution.py:639
  390.8 0.0 copy-start
  390.8 1.2 copy-done
  392.0 0.0 copy-start.1
  392.0 1.2 copy-done.1
  393.2 0.0 copy-start.3
  393.2 0.0 copy-start.2
  393.2 63.7 %grads.1 = (f32[2,1,1024,256]{3,2,1,0:T(8,128)S(1)}, f32[2,1,256,1024]{3,2,1,0:T(8,128)S(1)}) custom-call(bf16[2,16,8,32,1024]{4,3,2,1,0:T(8,128)(2,1)} %bitcast.2, bf16[2,16,8,32,1024]{4,3,2,1,0:T(8,128)(2,1)} %bitcast.3, bf16[2,4,256,256]{3,2,1,0:T(8,128)(2,1)S(1)} %copy-done, bf16[2,4,256,256]{3,2,1,0:T(8,128)(2,1)S(1)} %copy-done.1), custom_call_target="tpu_custom_call" | custom-call | tf_op jit(solution)/shard_map/grads/pallas_call | solution.py:670
  456.9 0.0 copy-done.3
  456.9 0.6 copy.12
  457.6 0.0 copy-done.2
  457.6 0.6 copy.13
  458.2 1.3 copy.14
  459.5 1.3 copy.15
Async XLA Ops:
  390.8 1.2 copy-start
  392.0 1.2 copy-start.1
  393.2 63.7 %copy-start.3 = (bf16[1,32,1024]{2,1,0:T(8,128)(2,1)S(1)}, bf16[1,32,1024]{2,1,0:T(8,128)(2,1)}, u32[]{:S(2)}) copy-start(bf16[1,32,1024]{2,1,0:T(8,128)(2,1)} %get-tuple-element.24) | copy-start | bytes 196612
  393.2 64.3 %copy-start.2 = (bf16[1,32,1024]{2,1,0:T(8,128)(2,1)S(1)}, bf16[1,32,1024]{2,1,0:T(8,128)(2,1)}, u32[]{:S(2)}) copy-start(bf16[1,32,1024]{2,1,0:T(8,128)(2,1)} %get-tuple-element.25) | copy-start | bytes 196612
